TPU v7x, 256 devices: a whole 4x4x8 slice. The times are simulated.
256 devices in a mesh: row: 8 (over y, core), col: 32 (over x, z).
Axes of the slice: x: 4, y: 4, z: 8, core: 2. Of those that a mesh axis runs over, the one named last changes fastest.
Arguments:
- matrix: float32 [4096, 4096], P('row', 'col'), may hold values from -12 to 12, as said below
Outputs:
- sign_estimate: float32 [4096, 4096], P('row', 'col')
Inputs may be any that keep to these rules, and one draw needn't show every extreme that they name: `matrix`: symmetric; the magnitudes of its eigenvalues, divided by the root mean square of all its eigenvalues, lie between 0.4 and 1.7.
All inputs are finite; a program needn't handle non-finite values.
Results may differ from a plain program's by a relative error of at most 0.0002.
Values sent between devices are 32-bit elements; how exact they have to be, the bound alone decides.
A program may use at most 64 MiB of HBM per device.

v0:
```python
import jax
import jax.numpy as jnp
from jax import lax
from jax.sharding import Mesh
from jax.sharding import PartitionSpec as P

N = 4096
ITERS = 2
ROW_COL = ("row_0", "row_1", "col_0", "col_1")
COL = ("col_0", "col_1")
ROW = ("row_0", "row_1")


def by_axis(array, axes):
    for axis in axes:
        array = lax.psum(array, axis)
    return array


def joined_along(tiles, dim):
    tiles = jnp.moveaxis(tiles, 0, dim)
    lengths = tiles.shape
    return tiles.reshape(*lengths[:dim], lengths[dim] * lengths[dim + 1], *lengths[dim + 2 :])


def sent_to_all(array, axis):
    copies = jnp.broadcast_to(array, (lax.axis_size(axis), *array.shape))
    return lax.all_to_all(copies, axis, split_axis=0, concat_axis=0, tiled=True)


def collect(array, axis, dim):
    return joined_along(sent_to_all(array, axis), dim)


def shards(matrix):
    total = by_axis(jnp.sum(matrix * matrix), ROW_COL)
    factor = jnp.sqrt(N / total)
    x_iter = matrix * factor
    for step in range(ITERS):
        delayed = step == 0
        source = matrix if delayed else x_iter
        rows_panel = lax.all_gather(source, COL, axis=1, tiled=True)
        cols_panel = collect(source, ROW, 0)
        square = jnp.dot(
            rows_panel,
            cols_panel,
            preferred_element_type=jnp.float32,
            precision=lax.Precision.HIGHEST,
        )
        if delayed:
            square = square * (factor * factor)
        cube_block = jnp.dot(
            rows_panel,
            collect(square, ROW, 0),
            preferred_element_type=jnp.float32,
            precision=lax.Precision.HIGHEST,
        )
        if delayed:
            cube_block = cube_block * factor
        x_iter = 1.5 * x_iter - 0.5 * cube_block
    return x_iter


def solution(mesh):
    split = Mesh(mesh.devices.reshape(4, 2, 4, 8), ("row_0", "row_1", "col_0", "col_1"))
    in_specs = (P(ROW, COL),)
    out_specs = P(ROW, COL)
    return jax.shard_map(
        shards, mesh=split, in_specs=in_specs, out_specs=out_specs, check_vma=False
    )
```

profile of v0, /device:TPU:1, one launch (start us, length us, event | category | flops | bytes accessed | tf_op | source)
XLA Modules:
  0.0 325.3 jit_solution(318392575473456364)
XLA Ops:
  6.5 0.0 all-gather.3.cloned.1.call-start
  6.5 0.7 all-gather.3.cloned.1.call-update
  7.3 2.5 broadcast_in_dim.12
  9.7 0.0 copy-start.2
  9.7 6.8 %all-to-all-start = ((f32[8,512,128]{2,1,0:T(8,128)}), f32[8,512,128]{2,1,0:T(8,128)S(1)}, u32[]{:S(2)}, u32[]{:S(2)}) async-start(f32[8,512,128]{2,1,0:T(8,128)} %broadcast_in_dim.12), calls=%async_computation | async-start | bytes 4194304 | tf_op jit(solution)/shard_map/all_to_all | solution.py:28
  16.6 0.0 copy-done.2
  16.6 0.7 multiply_reduce_fusion
  17.2 27.5 %psum.28 = f32[]{:T(128)} all-reduce(f32[]{:T(128)} %multiply_reduce_fusion), channel_id=1, replica_groups=mesh['row_0'=4,'row_1'=2,'col_0'=4,'col_1'=8] {'row_0'}, use_global_device_ids=true, to_apply=%region_1.0 | all-reduce | flops 1 | bytes 8 | tf_op jit(solution)/shard_map/psum | solution.py:16
  44.7 4.6 %psum.29 = f32[]{:T(128)} all-reduce(f32[]{:T(128)} %psum.28), channel_id=1, replica_groups=mesh['row_0'=4,'row_1'=2,'col_0'=4,'col_1'=8] {'row_1'}, use_global_device_ids=true, to_apply=%region_2.0 | all-reduce | flops 1 | bytes 8 | tf_op jit(solution)/shard_map/psum | solution.py:16
  49.3 8.7 %psum.30 = f32[]{:T(128)} all-reduce(f32[]{:T(128)} %psum.29), channel_id=1, replica_groups=mesh['row_0'=4,'row_1'=2,'col_0'=4,'col_1'=8] {'col_0'}, use_global_device_ids=true, to_apply=%region_3.0 | all-reduce | flops 1 | bytes 8 | tf_op jit(solution)/shard_map/psum | solution.py:16
  58.0 17.8 %psum.31 = f32[]{:T(128)} all-reduce(f32[]{:T(128)} %psum.30), channel_id=1, replica_groups=mesh['row_0'=4,'row_1'=2,'col_0'=4,'col_1'=8] {'col_1'}, use_global_device_ids=true, to_apply=%region_4.0 | all-reduce | flops 1 | bytes 8 | tf_op jit(solution)/shard_map/psum | solution.py:16
  76.5 0.0 all-to-all-done
  76.5 36.1 %all-gather.3.cloned.1.call-done = f32[512,4096]{1,0:T(8,128)} async-done(((f32[512,128]{1,0:T(8,128)}), f32[512,4096]{1,0:T(8,128)}) %all-gather.3.cloned.1.call-update) | async-done | bytes 8388624 | tf_op jit(solution)/shard_map/all_gather | solution.py:42
  112.6 9.1 %convolution_multiply_fusion.2 = f32[512,128]{1,0:T(8,128)S(1)} fusion(f32[512,4096]{1,0:T(8,128)} %all-gather.3.cloned.1.call-done, f32[4096,128]{1,0:T(8,128)S(1)} %bitcast.16, f32[]{:T(128)S(6)} %mul.44), kind=kOutput, calls=%fused_computation.5 | convolution fusion | flops 3221291008 | bytes 10747908 | tf_op jit(solution)/shard_map/dot_general | solution.py:44
  121.7 1.5 broadcast_in_dim.13
  123.2 8.1 %all-to-all-start.1 = ((f32[8,512,128]{2,1,0:T(8,128)}), f32[8,512,128]{2,1,0:T(8,128)S(1)}, u32[]{:S(2)}, u32[]{:S(2)}) async-start(f32[8,512,128]{2,1,0:T(8,128)} %broadcast_in_dim.13), calls=%async_computation.1 | async-start | bytes 4194304 | tf_op jit(solution)/shard_map/all_to_all | solution.py:28
  131.4 0.0 all-gather.5.cloned.1.call-start
  131.4 0.1 copy.2
  131.5 26.1 %all-to-all-done.1 = f32[8,512,128]{2,1,0:T(8,128)S(1)} async-done(((f32[8,512,128]{2,1,0:T(8,128)}), f32[8,512,128]{2,1,0:T(8,128)S(1)}, u32[]{:S(2)}, u32[]{:S(2)}) %all-to-all-start.1) | async-done | bytes 2097184 | tf_op jit(solution)/shard_map/all_to_all | solution.py:28
  157.6 11.8 %fusion.3 = f32[512,128]{0,1:T(8,128)} fusion(f32[4096,128]{1,0:T(8,128)S(1)} %bitcast.17, f32[512,4096]{1,0:T(8,128)} %all-gather.3.cloned.1.call-done, f32[512,128]{0,1:T(8,128)S(1)} %copy.2, f32[]{:T(128)S(6)} %sqrt.3), kind=kOutput, calls=%fused_computation.6 | convolution fusion | flops 3221553152 | bytes 11010052 | tf_op jit(solution)/shard_map/dot_general | solution.py:52
  169.4 0.0 all-gather.5.cloned.1.call-update
  169.4 1.1 copy.3
  170.5 0.1 broadcast_in_dim.14
  170.7 29.6 %all_to_all.20 = f32[8,512,128]{2,1,0:T(8,128)S(1)} all-to-all(f32[8,512,128]{2,1,0:T(8,128)S(1)} %broadcast_in_dim.14), channel_id=1, replica_groups=mesh['row_0'=4,'row_1'=2,'col_0'=4,'col_1'=8] {'row_0','row_1'}, dimensions={0} | all-to-all | bytes 4194304 | tf_op jit(solution)/shard_map/all_to_all | solution.py:28
  200.3 64.2 %all-gather.5.cloned.1.call-done = f32[512,4096]{0,1:T(8,128)} async-done(((f32[512,128]{0,1:T(8,128)}), f32[512,4096]{0,1:T(8,128)}) %all-gather.5.cloned.1.call-update) | async-done | bytes 8388624 | tf_op jit(solution)/shard_map/all_gather | solution.py:42
  264.4 0.0 copy-start
  264.4 15.7 %fusion.4 = f32[512,128]{1,0:T(8,128)S(1)} fusion(f32[512,4096]{0,1:T(8,128)} %all-gather.5.cloned.1.call-done, f32[4096,128]{1,0:T(8,128)S(1)} %bitcast.18), kind=kOutput, calls=%fused_computation.8 | convolution fusion | flops 3221225472 | bytes 10747904 | tf_op jit(solution)/shard_map/dot_general | solution.py:44
  280.1 0.1 broadcast_in_dim.15
  280.2 0.0 copy-start.1
  280.2 31.8 %all_to_all.21 = f32[8,512,128]{2,1,0:T(8,128)S(1)} all-to-all(f32[8,512,128]{2,1,0:T(8,128)S(1)} %broadcast_in_dim.15), channel_id=1, replica_groups=mesh['row_0'=4,'row_1'=2,'col_0'=4,'col_1'=8] {'row_0','row_1'}, dimensions={0} | all-to-all | bytes 4194304 | tf_op jit(solution)/shard_map/all_to_all | solution.py:28
  312.0 0.0 copy-done
  312.0 0.0 copy-done.1
  312.0 5.6 %fusion = f32[512,128]{0,1:T(8,128)S(1)} fusion(f32[512,4096]{0,1:T(8,128)S(1)} %copy-done, f32[4096,128]{1,0:T(8,128)S(1)} %bitcast.19, f32[512,128]{0,1:T(8,128)S(1)} %copy-done.1), kind=kOutput, calls=%fused_computation.1 | convolution fusion | flops 3221422080 | bytes 11010048 | tf_op jit(solution)/shard_map/dot_general | solution.py:52
  317.6 0.8 copy.5
Async XLA Ops:
  6.5 106.0 %all-gather.3.cloned.1.call-start = ((), (), s32[]{:S(2)}) async-start(), calls=%async_computation.4 | async-start | bytes 8650752 | tf_op jit(solution)/shard_map/all_gather | solution.py:42
  9.7 6.8 %copy-start.2 = (f32[512,128]{1,0:T(8,128)S(1)}, f32[512,128]{1,0:T(8,128)}, u32[]{:S(2)}) copy-start(f32[512,128]{1,0:T(8,128)} %param.1) | copy-start | bytes 786436
  9.7 66.7 %all-to-all-start = ((f32[8,512,128]{2,1,0:T(8,128)}), f32[8,512,128]{2,1,0:T(8,128)S(1)}, u32[]{:S(2)}, u32[]{:S(2)}) async-start(f32[8,512,128]{2,1,0:T(8,128)} %broadcast_in_dim.12), calls=%async_computation | async-start | bytes 4194304 | tf_op jit(solution)/shard_map/all_to_all | solution.py:28
  123.2 34.4 %all-to-all-start.1 = ((f32[8,512,128]{2,1,0:T(8,128)}), f32[8,512,128]{2,1,0:T(8,128)S(1)}, u32[]{:S(2)}, u32[]{:S(2)}) async-start(f32[8,512,128]{2,1,0:T(8,128)} %broadcast_in_dim.13), calls=%async_computation.1 | async-start | bytes 4194304 | tf_op jit(solution)/shard_map/all_to_all | solution.py:28
  131.4 133.0 %all-gather.5.cloned.1.call-start = ((), (), s32[]{:S(2)}) async-start(), calls=%async_computation.5 | async-start | bytes 8650752 | tf_op jit(solution)/shard_map/all_gather | solution.py:42
  264.4 47.6 %copy-start = (f32[512,4096]{0,1:T(8,128)S(1)}, f32[512,4096]{0,1:T(8,128)}, u32[]{:S(2)}) copy-start(f32[512,4096]{0,1:T(8,128)} %all-gather.5.cloned.1.call-done) | copy-start | bytes 25165828
  280.2 31.8 %copy-start.1 = (f32[512,128]{0,1:T(8,128)S(1)}, f32[512,128]{0,1:T(8,128)}, u32[]{:S(2)}) copy-start(f32[512,128]{0,1:T(8,128)} %fusion.3) | copy-start | bytes 786436
Sparse Core Ops, SparseCore 0:
  9.8 102.7 all-gather.2
  169.6 94.8 all-gather.4
where the time goes:
time: 326 us; the launch traced here: 325 us
  waiting for transfers between devices  127 us (39%)
  blocking collectives  120 us (37%)
  matrix products  42.2 us (13%)
  starting transfers between devices  15 us (5%)
  between operations  14.2 us (4%)
  local copies, waits for them, and re-layouts  6.33 us (2%)
    all_gather x2, waiting for transfers between devices, shards(): rows_panel = lax.all_gather(source, COL, axis=1, tiled=True)  100 us
    all_to_all x2, blocking collectives, sent_to_all(): return lax.all_to_all(copies, axis, split_axis=0, concat_axis=0, tiled=True)  61.4 us
    psum x4, blocking collectives, by_axis(): array = lax.psum(array, axis)  58.5 us
    all_to_all x2, waiting for transfers between devices, sent_to_all(): return lax.all_to_all(copies, axis, split_axis=0, concat_axis=0, tiled=True)  26.1 us
    dot_general x2, matrix products, shards(): jnp.dot(rows_panel, cols_panel, preferred_element_type=jnp.float32, preci...  24.8 us
    dot_general x2, matrix products, shards(): jnp.dot(rows_panel, collect(square, ROW, 0), preferred_element_type=jnp.f...  17.4 us
    all_to_all x2, starting transfers between devices, sent_to_all(): return lax.all_to_all(copies, axis, split_axis=0, concat_axis=0, tiled=True)  15 us
  transfers between devices with their start and end apart: 4, of which 3 were waited for; matrix products, arithmetic and copies ran while one was open for 1% of the time, Pallas kernels for 0%

commit v1 on v0

v1 whole, which is shorter than its diff:
```python
import functools

import jax
import jax.numpy as jnp
from jax import lax
from jax.experimental import pallas as pl
from jax.experimental.pallas import tpu as pltpu
from jax.sharding import Mesh
from jax.sharding import PartitionSpec as P

N = 4096
ITERS = 2
NY, NC, NX, NZ = 4, 2, 4, 8
ROWS = N // (NY * NC)
STRIP = N // (NX * NZ)
HALF = ROWS // 2
QROWS = STRIP // (2 * NY)
GROUPS = ((0, 3), (3, 2), (5, 2), (7, 1))
BF = jnp.bfloat16
F32 = jnp.float32


def split(value):
    high = value.astype(BF)
    return high, (value - high.astype(F32)).astype(BF)


def three(dot, a, b):
    return dot(a[0], b[0]) + (dot(a[0], b[1]) + dot(a[1], b[0]))


def dot_nn(a, b):
    return lax.dot_general(a, b, (((1,), (0,)), ((), ())), preferred_element_type=F32)


def dot_tn(a, b):
    return lax.dot_general(a, b, (((0,), (0,)), ((), ())), preferred_element_type=F32)


def kernel(
    m_ref, o_ref,
    block, panel, block_hi, block_lo, panel_hi, panel_lo,
    part, from_core, mine, chain, ended, square, cube, x_chain, x_ended, factor, sums_x, sums_y,
    z_send, z_recv, x_send, x_recv, g_send, g_recv, s_send, s_recv,
):
    y, c, x, z = (lax.axis_index(name) for name in ("y", "c", "x", "z"))

    def turn(name, here, by, size):
        return {name: lax.rem(here + by, size)}

    up_z, down_z = turn("z", z, 1, NZ), turn("z", z, NZ - 1, NZ)
    up_x, down_x = turn("x", x, 1, NX), turn("x", x, NX - 1, NX)
    up_y, down_y = turn("y", y, 1, NY), turn("y", y, NY - 1, NY)
    other_core = {"c": 1 - c}
    x_peers = [turn("x", x, d, NX) for d in range(1, NX)]
    y_peers = [{"y": lax.rem(y + d, NY), "c": lax.rem(c + e, NC)} for d in range(NY) for e in range(NC)][1:]

    barrier = pltpu.get_barrier_semaphore()
    peers = [up_z, down_z, *x_peers, *y_peers]
    for peer in peers:
        pl.semaphore_signal(barrier, inc=1, device_id=peer, device_id_type=pl.DeviceIdType.MESH)

    pending = []

    def copy(src, dst, send, recv, peer):
        return pltpu.make_async_remote_copy(
            src_ref=src, dst_ref=dst, send_sem=send, recv_sem=recv,
            device_id=peer, device_id_type=pl.DeviceIdType.MESH,
        )

    def go(made):
        made.start()
        pending.append(made)

    def quarter(by):
        return lax.rem(y + by, NY)

    for it in range(ITERS):
        block_i, panel_i = block.at[it], panel.at[it]

        def z_copy(src_pos, dst_pos, piece, peer):
            rows = pl.ds(piece * HALF, HALF)
            return copy(
                block_i.at[src_pos, rows], block_i.at[dst_pos, rows],
                z_send.at[it, dst_pos, piece], z_recv.at[it, dst_pos, piece], peer,
            )

        ups = {(p, q): z_copy({2: 0, 4: 2, 6: 4}[p], p, q, up_z) for p in (2, 4, 6) for q in (0, 1)}
        downs = {(p, q): z_copy({1: 0, 3: 1, 5: 3}[p], p, q, down_z) for p in (1, 3, 5) for q in (0, 1)}
        ups[7, 0] = z_copy(6, 7, 0, up_z)
        downs[7, 1] = z_copy(5, 7, 1, down_z)

        def x_copy(src, dst, piece, k, peer):
            rows = pl.ds(piece * HALF, HALF)
            return copy(src.at[rows], panel_i.at[dst, rows], x_send.at[it, k], x_recv.at[it, k], peer)

        own = block_i.at[0]
        x_up = [x_copy(own, 3, 0, 0, up_x), x_copy(own, 3, 1, 1, up_x)]
        x_down = [x_copy(own, 1, 0, 2, down_x), x_copy(own, 1, 1, 3, down_x)]
        x_up_far = x_copy(panel_i.at[3], 2, 0, 4, up_x)
        x_down_far = x_copy(panel_i.at[1], 2, 1, 5, down_x)

        def start_all():
            if it == 0:
                block_i[0] = m_ref[...]
                pl.semaphore_wait(barrier, len(peers))
            for q in (0, 1):
                go(x_up[q])
                go(x_down[1 - q])
                go(ups[2, q])
                go(downs[1, q])
            put_panel(0, block_i[0])
            put_block(0)

        def put_panel(slot, value):
            columns = slice(slot * STRIP, (slot + 1) * STRIP)
            panel_hi[:, columns], panel_lo[:, columns] = split(value)

        def put_block(pos):
            columns = slice(pos * STRIP, (pos + 1) * STRIP)
            block_hi[:, columns], block_lo[:, columns] = split(block_i[pos])

        def z_step(pos, piece):
            downs[pos, piece].wait_recv()
            if (pos + 2, piece) in downs:
                go(downs[pos + 2, piece])
            ups[pos + 1, piece].wait_recv()
            if (pos + 3, piece) in ups:
                go(ups[pos + 3, piece])
            if pos == 5 and piece == 0:
                go(ups[7, 0])
            if piece == 1:
                put_block(pos)
                put_block(pos + 1)

        def z_last():
            ups[7, 0].wait_recv()
            downs[7, 1].wait_recv()
            put_block(7)

        def x_far():
            x_up[0].wait_recv()
            go(x_up_far)
            x_down[1].wait_recv()
            go(x_down_far)

        def x_near():
            x_up[1].wait_recv()
            x_down[0].wait_recv()
            put_panel(3, panel_i[3])
            put_panel(1, panel_i[1])

        def x_last():
            x_up_far.wait_recv()
            x_down_far.wait_recv()
            put_panel(2, panel_i[2])

        def group_copies(g):
            first, n = GROUPS[g]
            run = pl.ds(first, n)

            def made(k, src, dst, peer):
                return copy(src, dst, g_send.at[it, g, k], g_recv.at[it, g, k], peer)

            low, high = pl.ds(0, QROWS // 2), pl.ds(QROWS // 2, QROWS // 2)
            w, r1, r2, s = mine.at[it, run], chain.at[it, run], ended.at[it, run], square.at[it, run]
            at = lambda ref, *where: ref.at[(slice(None), *where)]
            return dict(
                core=made(0, at(part.at[it, run], 1 - c), from_core.at[it, run], other_core),
                chain_up=made(1, at(w, quarter(2), low), at(r1, 0), up_y),
                chain_down=made(2, at(w, quarter(2), high), at(r1, 1), down_y),
                near_down=made(3, at(w, quarter(3), low), at(r1, 2), down_y),
                near_up=made(4, at(w, quarter(1), high), at(r1, 3), up_y),
                end_up=made(5, at(w, quarter(1), low), at(r2, 0), up_y),
                end_down=made(6, at(w, quarter(3), high), at(r2, 1), down_y),
                give_up=made(7, at(s, c, y), at(s, c, y), up_y),
                give_down=made(8, at(s, c, y), at(s, c, y), down_y),
                far_up=made(9, at(s, c, quarter(3), low), at(s, c, quarter(3), low), up_y),
                far_down=made(10, at(s, c, quarter(1), high), at(s, c, quarter(1), high), down_y),
                join=made(11, at(s, c), at(s, c), other_core),
            )

        def multiply(g, cs):
            first, n = GROUPS[g]
            columns = slice(first * STRIP, (first + n) * STRIP)
            a = block_hi[:, columns], block_lo[:, columns]
            got = three(dot_tn, a, (panel_hi[...], panel_lo[...]))
            part[it, first : first + n] = got.reshape(n, NC, NY * QROWS, NX * STRIP)
            go(cs["core"])

        def step1(g, cs):
            first, n = GROUPS[g]
            cs["core"].wait_recv()
            for p in range(first, first + n):
                total = part[it, p, c] + from_core[it, p]
                mine[it, p] = total.reshape(NY, QROWS, NX * STRIP)
            for name in ("chain_up", "chain_down", "near_up", "near_down"):
                go(cs[name])

        def step2(g, cs):
            first, n = GROUPS[g]
            h = QROWS // 2
            cs["chain_up"].wait_recv()
            for p in range(first, first + n):
                mine[it, p, quarter(1), 0:h] += chain[it, p, 0]
            go(cs["end_up"])
            cs["chain_down"].wait_recv()
            for p in range(first, first + n):
                mine[it, p, quarter(3), h : 2 * h] += chain[it, p, 1]
            go(cs["end_down"])

        def step3(g, cs):
            first, n = GROUPS[g]
            h = QROWS // 2
            for name in ("near_down", "near_up", "end_up", "end_down"):
                cs[name].wait_recv()
            for p in range(first, first + n):
                square[it, p, c, y, 0:h] = mine[it, p, y, 0:h] + (ended[it, p, 0] + chain[it, p, 2])
                square[it, p, c, y, h : 2 * h] = mine[it, p, y, h : 2 * h] + (ended[it, p, 1] + chain[it, p, 3])
            go(cs["give_up"])
            go(cs["give_down"])

        def step4(g, cs):
            cs["give_up"].wait_recv()
            go(cs["far_up"])
            cs["give_down"].wait_recv()
            go(cs["far_down"])

        def step5(g, cs):
            cs["far_up"].wait_recv()
            cs["far_down"].wait_recv()
            go(cs["join"])

        def step6(g, cs):
            first, n = GROUPS[g]
            cs["join"].wait_recv()
            value = square[it, first : first + n].reshape(n * STRIP, NX * STRIP)
            if it == 0:
                f = factor[0:1, 0:1]
                value = value * (f * f)
            columns = slice(first * STRIP, (first + n) * STRIP)
            a = block_hi[:, columns], block_lo[:, columns]
            got = three(dot_nn, a, split(value))
            for d in range(NX):
                piece = got[:, d * STRIP : (d + 1) * STRIP]
                if g == 0:
                    cube[it, d] = piece
                else:
                    cube[it, d] += piece

        def sums1():
            tile = jnp.zeros((8, 128), F32)
            for p in range(NZ):
                v = block_i[p].reshape(ROWS // 8, 8, STRIP)
                tile = tile + jnp.sum(v * v, axis=0)
            sums_x[0] = tile
            for k in range(1, NX):
                go(sx[k])

        def sums2():
            for k in range(1, NX):
                sx[k].wait_recv()
            sums_y[0] = (sums_x[0] + sums_x[1]) + (sums_x[2] + sums_x[3])
            for k in range(1, NY * NC):
                go(sy[k])

        def sums3():
            for k in range(1, NY * NC):
                sy[k].wait_recv()
            total = jnp.sum(jnp.sum(sums_y[...], axis=0), keepdims=True)
            factor[...] = jnp.broadcast_to(jnp.sqrt(N / total), factor.shape)

        sx = {k: copy(sums_x.at[0], sums_x.at[k], s_send.at[k], s_recv.at[k], x_peers[k - 1])
            for k in (range(1, NX) if it == 0 else ())}
        sy = {
            k: copy(sums_y.at[0], sums_y.at[k], s_send.at[NX + k], s_recv.at[NX + k], y_peers[k - 1])
            for k in (range(1, NY * NC) if it == 0 else ())
        }

        cs = [group_copies(g) for g in range(len(GROUPS))]
        low, high = pl.ds(0, HALF), pl.ds(HALF, HALF)

        def r_copy(k, src, dst, peer):
            return copy(src, dst, x_send.at[it, 6 + k], x_recv.at[it, 6 + k], peer)

        cb = cube.at[it]
        r_chain_up = r_copy(0, cb.at[2, low], x_chain.at[it, 0], up_x)
        r_chain_down = r_copy(1, cb.at[2, high], x_chain.at[it, 1], down_x)
        r_near_down = r_copy(2, cb.at[3, low], x_chain.at[it, 2], down_x)
        r_near_up = r_copy(3, cb.at[1, high], x_chain.at[it, 3], up_x)
        r_end_up = r_copy(4, cb.at[1, low], x_ended.at[it, 0], up_x)
        r_end_down = r_copy(5, cb.at[3, high], x_ended.at[it, 1], down_x)

        def finish():
            go(r_chain_up)
            go(r_chain_down)
            go(r_near_down)
            go(r_near_up)
            r_chain_up.wait_recv()
            cube[it, 1, 0:HALF] += x_chain[it, 0]
            go(r_end_up)
            r_chain_down.wait_recv()
            cube[it, 3, HALF:ROWS] += x_chain[it, 1]
            go(r_end_down)
            r_near_down.wait_recv()
            r_near_up.wait_recv()
            for k, (end, rows) in enumerate(((r_end_up, slice(0, HALF)), (r_end_down, slice(HALF, ROWS)))):
                end.wait_recv()
                product = cube[it, 0, rows] + (x_ended[it, k] + x_chain[it, 2 + k])
                value = block_i[0, rows]
                if it == 0:
                    f = factor[0:1, 0:1]
                    new = (1.5 * f) * value - (0.5 * f) * product
                else:
                    new = 1.5 * value - 0.5 * product
                if it == ITERS - 1:
                    o_ref[rows] = new
                else:
                    block[it + 1, 0, rows] = new

        events = [
            (0.0, start_all),
            (4.5, functools.partial(z_step, 1, 0)),
            (4.6, x_far),
            (7.2, functools.partial(z_step, 1, 1)),
            (7.3, x_near),
            (10.0, functools.partial(z_step, 3, 0)),
            (10.1, x_last),
            (12.9, functools.partial(z_step, 3, 1)),
            (15.7, functools.partial(z_step, 5, 0)),
            (18.5, functools.partial(z_step, 5, 1)),
            (21.3, z_last),
        ]
        stages = (multiply, step1, step2, step3, step4, step5, step6)
        times = (
            (10.5, 13.0, 16.9, 19.8, 23.0, 26.0, 27.5),
            (12.95, 14.8, 18.4, 20.6, 24.0, 27.0, 28.6),
            (18.6, 20.4, 22.6, 25.0, 27.2, 29.2, 30.8),
            (21.4, 23.5, 25.5, 28.0, 30.0, 32.0, 33.5),
        )
        for g in range(len(GROUPS)):
            for stage, when in zip(stages, times[g]):
                events.append((when, functools.partial(stage, g, cs[g])))
        if it == 0:
            events += [(21.5, sums1), (24.1, sums2), (27.1, sums3)]
        events.append((40.0, finish))
        for _, do in sorted(events, key=lambda e: e[0]):
            do()

    for made in pending:
        made.wait_send()


def shards(matrix):
    dma = pltpu.SemaphoreType.DMA
    wide = NX * STRIP
    return pl.pallas_call(
        kernel,
        out_shape=jax.ShapeDtypeStruct((ROWS, STRIP), F32),
        in_specs=[pl.BlockSpec(memory_space=pltpu.VMEM)],
        out_specs=pl.BlockSpec(memory_space=pltpu.VMEM),
        scratch_shapes=[
            pltpu.VMEM((ITERS, NZ, ROWS, STRIP), F32),
            pltpu.VMEM((ITERS, NX, ROWS, STRIP), F32),
            pltpu.VMEM((ROWS, NZ * STRIP), BF),
            pltpu.VMEM((ROWS, NZ * STRIP), BF),
            pltpu.VMEM((ROWS, wide), BF),
            pltpu.VMEM((ROWS, wide), BF),
            pltpu.VMEM((ITERS, NZ, NC, STRIP // 2, wide), F32),
            pltpu.VMEM((ITERS, NZ, STRIP // 2, wide), F32),
            pltpu.VMEM((ITERS, NZ, NY, QROWS, wide), F32),
            pltpu.VMEM((ITERS, NZ, 4, QROWS // 2, wide), F32),
            pltpu.VMEM((ITERS, NZ, 2, QROWS // 2, wide), F32),
            pltpu.VMEM((ITERS, NZ, NC, NY, QROWS, wide), F32),
            pltpu.VMEM((ITERS, NX, ROWS, STRIP), F32),
            pltpu.VMEM((ITERS, 4, HALF, STRIP), F32),
            pltpu.VMEM((ITERS, 2, HALF, STRIP), F32),
            pltpu.VMEM((8, 128), F32),
            pltpu.VMEM((NX, 8, 128), F32),
            pltpu.VMEM((NY * NC, 8, 128), F32),
            dma((ITERS, NZ, 2)),
            dma((ITERS, NZ, 2)),
            dma((ITERS, 12)),
            dma((ITERS, 12)),
            dma((ITERS, len(GROUPS), 12)),
            dma((ITERS, len(GROUPS), 12)),
            dma((NX + NY * NC,)),
            dma((NX + NY * NC,)),
        ],
        compiler_params=pltpu.CompilerParams(
            collective_id=0, has_side_effects=True, vmem_limit_bytes=56 * 1024 * 1024
        ),
    )(matrix)


def solution(mesh):
    grid = Mesh(mesh.devices.reshape(NY, NC, NX, NZ), ("y", "c", "x", "z"))
    spec = P(("y", "c"), ("x", "z"))
    return jax.shard_map(shards, mesh=grid, in_specs=(spec,), out_specs=spec, check_vma=False)
```

time: 326 us -> 124 us (0.38)
  waiting for transfers between devices: 127 us -> 0 us
  Pallas kernels: 0 us -> 122 us
  blocking collectives: 120 us -> 0 us
  matrix products: 42.2 us -> 0 us
  starting transfers between devices: 15 us -> 0 us
  between operations: 14.2 us -> 0.01 us
  local copies, waits for them, and re-layouts: 6.33 us -> 1.67 us
    pallas_call x0 -> x1, Pallas kernels: none -> 122 us  [shards(): pl.pallas_call(kernel, out_shape=jax.ShapeDtypeStruct((ROWS, STRIP), F32)...]
    all_gather x2 -> x0, waiting for transfers between devices: 100 us -> none  [shards(): rows_panel = lax.all_gather(source, COL, axis=1, tiled=True)]
    all_to_all x2 -> x0, blocking collectives: 61.4 us -> none  [sent_to_all(): return lax.all_to_all(copies, axis, split_axis=0, concat_axis=0, tiled=True)]
    psum x4 -> x0, blocking collectives: 58.5 us -> none  [by_axis(): array = lax.psum(array, axis)]
    dot_general x4 -> x0, matrix products: 42.2 us -> none  [the longest x2 24.8 us: shards(): jnp.dot(rows_panel, cols_panel, preferred_element_type=jnp.float32, preci...]
    all_to_all x2 -> x0, waiting for transfers between devices: 26.1 us -> none  [sent_to_all(): return lax.all_to_all(copies, axis, split_axis=0, concat_axis=0, tiled=True)]
    all_to_all x2 -> x0, starting transfers between devices: 15 us -> none  [sent_to_all(): return lax.all_to_all(copies, axis, split_axis=0, concat_axis=0, tiled=True)]
    broadcast_in_dim x4 -> x0, local copies, waits for them, and re-layouts: 4.28 us -> none  [sent_to_all(): copies = jnp.broadcast_to(array, (lax.axis_size(axis), *array.shape))]
  transfers between devices with their start and end apart: 4 -> 0, of which waited for: 3 -> 0; matrix products, arithmetic and copies ran while one was open for 1% -> 0% of each run, Pallas kernels for 0% -> 0%
where the time goes in v1:
time: 124 us
  Pallas kernels  122 us (98%)
  local copies, waits for them, and re-layouts  1.67 us (1%)
    pallas_call x1, Pallas kernels, shards(): pl.pallas_call(kernel, out_shape=jax.ShapeDtypeStruct((ROWS, STRIP), F32)...  122 us

profile of v1, /device:TPU:1, one launch (start us, length us, event | category | flops | bytes accessed | tf_op | source)
XLA Modules:
  0.0 124.1 jit_solution(498767616118132432)
XLA Ops:
  0.0 122.4 %shard_map.17 = f32[512,128]{1,0:T(8,128)} custom-call(f32[512,128]{1,0:T(8,128)} %m_ref.1), custom_call_target="tpu_custom_call" | custom-call | tf_op jit(solution)/shard_map/pallas_call | solution.py:357
  122.4 1.7 %copy.3 = f32[512,128]{1,0:T(8,128)} copy(f32[512,128]{1,0:T(8,128)} %shard_map.17) | data formatting | bytes 524288

commit v2 on v0

v2 whole, which is shorter than its diff:
```python
import jax
import jax.numpy as jnp
from jax import lax
from jax.experimental import pallas as pl
from jax.experimental.pallas import tpu as pltpu
from jax.sharding import Mesh
from jax.sharding import PartitionSpec as P

N = 4096
ITERS = 2
NY, NC, NX, NZ = 4, 2, 4, 8
ROWS = N // (NY * NC)
STRIP = N // (NX * NZ)
HALF = ROWS // 2
SROWS = STRIP // NC
SHALF = SROWS // 2
GROUPS = ((0, 1), (1, 2), (3, 2), (5, 2), (7, 1))
SETS = ((2,), (1, 3), (0,))
LANES = ((0, 1), (1, 2), (3, 1))
BF = jnp.bfloat16
F32 = jnp.float32
ORDER = (
    (
        ("own",), ("put", 0), ("mul", 0, 2), ("s1", 0, 2), ("s2", 0, 2), ("zd", 1, 1, 0), ("zu", 2, 0, 0), ("xfu",),
        ("xfd",), ("s3", 0, 2), ("zu", 2, 1, 0), ("zd", 1, 0, 0), ("put", 2), ("put", 1), ("mul", 1, 2), ("xnear",),
        ("mul", 1, 1), ("mul", 0, 1), ("s1", 1, 2), ("s1", 1, 1), ("s1", 0, 1), ("zd", 3, 1, 0), ("zu", 4, 0, 0),
        ("xlast",), ("mul", 1, 0), ("sums1",), ("mul", 0, 0), ("s1", 1, 0), ("s1", 0, 0), ("s2", 1, 2),
        ("zu", 4, 1, 0), ("put", 4), ("zd", 3, 0, 0), ("put", 3), ("mul", 2), ("s2", 1, 1), ("s2", 0, 1),
        ("sums2",), ("s1", 2, 0), ("s1", 2, 1), ("s1", 2, 2), ("s2", 1, 0), ("zu", 6, 0, 0), ("zd", 5, 1, 0),
        ("s2", 0, 0), ("s3", 1, 2), ("s3", 1, 1), ("zu", 6, 1, 0), ("zd", 5, 0, 0), ("put", 5), ("put", 6),
        ("mul", 3), ("s3", 0, 1), ("s2", 2, 0), ("s1", 3, 0), ("s1", 3, 1), ("s1", 3, 2), ("s2", 2, 1), ("sums3",),
        ("put", 7), ("mul", 4), ("s2", 2, 2), ("s3", 1, 0), ("s3", 0, 0), ("s1", 4, 0), ("s1", 4, 1), ("s3", 2, 0),
        ("s1", 4, 2), ("s6", 0), ("s2", 3, 0), ("s6", 1), ("s2", 3, 1), ("s6", 2, 0), ("s2", 3, 2), ("s3", 2, 1),
        ("s3", 2, 2), ("s2", 4, 0), ("s6", 2, 1), ("s2", 4, 1), ("s6", 2, 2), ("s2", 4, 2), ("s3", 3, 0),
        ("s6", 3, 0), ("s3", 3, 1), ("s3", 3, 2), ("s3", 4, 0), ("s3", 4, 1), ("s6", 3, 1), ("s6", 4, 0), ("rc",),
        ("s3", 4, 2), ("s6", 3, 2), ("s6", 4, 1), ("rn",), ("s6", 4, 2), ("re",), ("fin",),
    ),
    (
        ("own",), ("put", 0), ("mul", 0, 2), ("s1", 0, 2), ("s2", 0, 2), ("zu", 2, 0, 0), ("zd", 1, 1, 0), ("xfu",),
        ("xfd",), ("s3", 0, 2), ("zu", 2, 1, 0), ("put", 2), ("zd", 1, 0, 0), ("put", 1), ("mul", 1, 2), ("xnear",),
        ("mul", 1, 1), ("mul", 0, 1), ("s1", 1, 2), ("s1", 1, 1), ("s1", 0, 1), ("zd", 3, 1, 0), ("zu", 4, 0, 0),
        ("xlast",), ("mul", 0, 0), ("mul", 1, 0), ("s1", 0, 0), ("s1", 1, 0), ("s2", 1, 2), ("zu", 4, 1, 0),
        ("put", 4), ("zd", 3, 0, 0), ("put", 3), ("mul", 2), ("s2", 1, 1), ("s2", 0, 1), ("s1", 2, 0), ("s2", 0, 0),
        ("s1", 2, 1), ("s1", 2, 2), ("zu", 6, 0, 0), ("zd", 5, 1, 0), ("s2", 1, 0), ("s3", 1, 2), ("s3", 1, 1),
        ("zd", 5, 0, 0), ("put", 5), ("zu", 6, 1, 0), ("put", 6), ("mul", 3), ("s3", 0, 1), ("s2", 2, 0),
        ("s3", 0, 0), ("s1", 3, 0), ("s1", 3, 1), ("s1", 3, 2), ("s6", 0), ("s2", 2, 1), ("put", 7), ("mul", 4),
        ("s2", 2, 2), ("s3", 1, 0), ("s3", 2, 0), ("s1", 4, 0), ("s1", 4, 1), ("s1", 4, 2), ("s6", 1), ("s2", 3, 0),
        ("s6", 2, 0), ("s2", 3, 1), ("s2", 3, 2), ("s3", 2, 1), ("s3", 2, 2), ("s2", 4, 0), ("s6", 2, 1),
        ("s2", 4, 1), ("s6", 2, 2), ("s2", 4, 2), ("s3", 3, 0), ("s6", 3, 0), ("s3", 3, 1), ("s3", 3, 2),
        ("s3", 4, 0), ("s3", 4, 1), ("s6", 3, 1), ("s6", 4, 0), ("rc",), ("s3", 4, 2), ("s6", 3, 2), ("s6", 4, 1),
        ("rn",), ("s6", 4, 2), ("re",), ("fin",),
    ),
)


def split(value):
    high = value.astype(BF)
    return high, (value - high.astype(F32)).astype(BF)


def three(dim, a, b):
    a = jnp.concatenate([a[0], a[1], a[0]], axis=dim)
    b = jnp.concatenate([b[0], b[0], b[1]], axis=0)
    return lax.dot_general(a, b, (((dim,), (0,)), ((), ())), preferred_element_type=F32)


def lanes_of(s):
    first, n = LANES[s]
    return slice(first * STRIP, (first + n) * STRIP)


def kernel(m_ref, o_ref, block, panel, block_hi, block_lo, panel_hi, panel_lo, square_hi, square_lo, *refs):
    ns = len(SETS)
    part, from_core, mine, first_in, ours, second_in, square = (refs[k * ns : (k + 1) * ns] for k in range(7))
    (
        cube, x_chain, x_ended, factor, sums_y, sums_z,
        z_send, z_recv, x_send, x_recv, g_send, g_recv, s_send, s_recv,
    ) = refs[7 * ns :]
    y, c, x, z = (lax.axis_index(name) for name in ("y", "c", "x", "z"))

    def turn(name, here, by, size):
        return {name: lax.rem(here + by, size)}

    up_z, down_z = turn("z", z, 1, NZ), turn("z", z, NZ - 1, NZ)
    up_x, down_x = turn("x", x, 1, NX), turn("x", x, NX - 1, NX)
    odd = lax.rem(y, 2)
    y_near, y_far = turn("y", y, NY + 1 - 2 * odd, NY), turn("y", y, NY - 1 + 2 * odd, NY)
    other_core = {"c": 1 - c}
    z_peers = [turn("z", z, d, NZ) for d in range(1, NZ)]
    y_peers = [{"y": lax.rem(y + d, NY), "c": lax.rem(c + e, NC)} for d in range(NY) for e in range(NC)][1:]

    barrier = pltpu.get_barrier_semaphore()
    peers = [up_x, down_x, *z_peers, *y_peers]
    for peer in peers:
        pl.semaphore_signal(barrier, inc=1, device_id=peer, device_id_type=pl.DeviceIdType.MESH)
    block[0, 0] = m_ref[...]
    pl.semaphore_wait(barrier, len(peers))

    pending = []

    def copy(src, dst, send, recv, peer):
        return pltpu.make_async_remote_copy(
            src_ref=src, dst_ref=dst, send_sem=send, recv_sem=recv,
            device_id=peer, device_id_type=pl.DeviceIdType.MESH,
        )

    def go(made):
        made.start()
        pending.append(made)

    low, high = pl.ds(0, SHALF), pl.ds(SHALF, SHALF)

    def iteration(it):
        block_i, panel_i, cube_i = block.at[it], panel.at[it], cube.at[it]

        def z_copy(src, dst, piece, peer):
            rows = pl.ds(piece * HALF, HALF)
            return copy(
                block_i.at[src, rows], block_i.at[dst, rows],
                z_send.at[it, dst, piece], z_recv.at[it, dst, piece], peer,
            )

        ups = {(p, q): z_copy(max(p - 2, 0), p, q, up_z) for p in (2, 4, 6) for q in (0, 1)}
        downs = {(p, q): z_copy(max(p - 2, 0), p, q, down_z) for p in (1, 3, 5) for q in (0, 1)}
        ups[8, 0] = z_copy(6, 7, 0, up_z)
        downs[7, 1] = z_copy(5, 7, 1, down_z)

        def x_copy(src, dst, piece, k, peer):
            rows = pl.ds(piece * HALF, HALF)
            return copy(src.at[rows], panel_i.at[dst, rows], x_send.at[it, k], x_recv.at[it, k], peer)

        own_strip = block_i.at[0]
        x_up = [x_copy(own_strip, 3, 0, 0, up_x), x_copy(own_strip, 3, 1, 1, up_x)]
        x_down = [x_copy(own_strip, 1, 0, 2, down_x), x_copy(own_strip, 1, 1, 3, down_x)]
        x_up_far = x_copy(panel_i.at[3], 2, 0, 4, up_x)
        x_down_far = x_copy(panel_i.at[1], 2, 1, 5, down_x)

        def put_panel(slot, value):
            at = {2: 0, 1: 1, 3: 2, 0: 3}[slot]
            columns = slice(at * STRIP, (at + 1) * STRIP)
            panel_hi[:, columns], panel_lo[:, columns] = split(value)

        def own():
            for q in (0, 1):
                go(x_up[q])
                go(x_down[1 - q])
                go(ups[2, q])
                go(downs[1, 1 - q])

        def zd(pos, piece, _):
            downs[pos, piece].wait_recv()
            if (pos + 2, piece) in downs:
                go(downs[pos + 2, piece])

        def zu(pos, piece, _):
            ups[pos, piece].wait_recv()
            if (pos + 2, piece) in ups:
                go(ups[pos + 2, piece])

        def put(pos):
            if pos == 7:
                ups[8, 0].wait_recv()
                downs[7, 1].wait_recv()
            columns = slice(pos * STRIP, (pos + 1) * STRIP)
            value = block[it, pos]
            block_hi[:, columns], block_lo[:, columns] = split(value)
            if pos == 0:
                put_panel(0, value)

        def xfu():
            x_up[0].wait_recv()
            go(x_up_far)

        def xfd():
            x_down[1].wait_recv()
            go(x_down_far)

        def xnear():
            x_up[1].wait_recv()
            x_down[0].wait_recv()
            put_panel(3, panel[it, 3])
            put_panel(1, panel[it, 1])

        def xlast():
            x_up_far.wait_recv()
            x_down_far.wait_recv()
            put_panel(2, panel[it, 2])

        def unit(g, s):
            run = pl.ds(*GROUPS[g])
            every = slice(None)

            def made(k, src, dst, peer):
                return copy(src, dst, g_send.at[it, g, s, k], g_recv.at[it, g, s, k], peer)

            def rows(ref, which):
                return ref[s].at[it, run, which]

            sums = square[s].at[it, run, c]
            return dict(
                core=made(0, part[s].at[it, run, 1 - c], from_core[s].at[it, run], other_core),
                low_one=made(1, rows(mine, low), rows(first_in, low), y_near),
                high_one=made(2, rows(mine, high), rows(first_in, high), y_far),
                low_two=made(3, rows(ours, low), rows(second_in, low), y_far),
                high_two=made(4, rows(ours, high), rows(second_in, high), y_near),
                join=made(5, sums, sums, other_core),
            )

        units = {(g, s): unit(g, s) for g in range(len(GROUPS)) for s in range(ns)}

        def strips(g):
            first, n = GROUPS[g]
            return range(first, first + n)

        def factors(g):
            first, n = GROUPS[g]
            columns = slice(first * STRIP, (first + n) * STRIP)
            return block_hi[:, columns], block_lo[:, columns]

        def mul(g, *which):
            first, n = GROUPS[g]
            columns = lanes_of(which[0]) if which else slice(0, NX * STRIP)
            got = three(0, factors(g), (panel_hi[:, columns], panel_lo[:, columns]))
            for s in which or range(ns):
                piece = got if which else got[:, lanes_of(s)]
                part[s][it, first : first + n] = piece.reshape(n, NC, SROWS, piece.shape[1])
                go(units[g, s]["core"])

        def s1(g, s):
            cs = units[g, s]
            cs["core"].wait_recv()
            for p in strips(g):
                mine[s][it, p] = part[s][it, p, c] + from_core[s][it, p]
            go(cs["low_one"])
            go(cs["high_one"])

        def s2(g, s):
            cs = units[g, s]
            for one, two, rows in (("low_one", "low_two", low), ("high_one", "high_two", high)):
                cs[one].wait_recv()
                for p in strips(g):
                    ours[s][it, p, rows] = mine[s][it, p, rows] + first_in[s][it, p, rows]
                go(cs[two])

        def s3(g, s):
            cs = units[g, s]
            cs["low_two"].wait_recv()
            cs["high_two"].wait_recv()
            for p in strips(g):
                square[s][it, p, c] = ours[s][it, p] + second_in[s][it, p]
            go(cs["join"])

        def s6(g, *which):
            first, n = GROUPS[g]
            rows = slice(first * STRIP, (first + n) * STRIP)
            todo = which or range(ns)
            for s in todo:
                units[g, s]["join"].wait_recv()
                value = square[s][it, first : first + n]
                value = value.reshape(n * STRIP, value.shape[-1])
                if it == 0:
                    f = factor[0:1, 0:1]
                    value = value * (f * f)
                square_hi[rows, lanes_of(s)], square_lo[rows, lanes_of(s)] = split(value)
            columns = lanes_of(which[0]) if which else slice(0, NX * STRIP)
            got = three(1, factors(g), (square_hi[rows, columns], square_lo[rows, columns]))
            for k, slot in enumerate([slot for s in todo for slot in SETS[s]]):
                piece = got[:, k * STRIP : (k + 1) * STRIP]
                if first == 0:
                    cube[it, slot] = piece
                else:
                    cube[it, slot] += piece

        def r_copy(k, src, dst, peer):
            return copy(src, dst, x_send.at[it, 6 + k], x_recv.at[it, 6 + k], peer)

        upper, lower = slice(0, HALF), slice(HALF, ROWS)
        r_chain_up = r_copy(0, cube_i.at[2, upper], x_chain.at[it, 0], up_x)
        r_chain_down = r_copy(1, cube_i.at[2, lower], x_chain.at[it, 1], down_x)
        r_near_down = r_copy(2, cube_i.at[3, upper], x_chain.at[it, 2], down_x)
        r_near_up = r_copy(3, cube_i.at[1, lower], x_chain.at[it, 3], up_x)
        r_end_up = r_copy(4, cube_i.at[1, upper], x_ended.at[it, 0], up_x)
        r_end_down = r_copy(5, cube_i.at[3, lower], x_ended.at[it, 1], down_x)

        def rc():
            go(r_chain_up)
            go(r_chain_down)

        def rn():
            go(r_near_up)
            go(r_near_down)

        def re():
            r_chain_up.wait_recv()
            cube[it, 1, upper] += x_chain[it, 0]
            go(r_end_up)
            r_chain_down.wait_recv()
            cube[it, 3, lower] += x_chain[it, 1]
            go(r_end_down)

        def fin():
            r_near_down.wait_recv()
            r_near_up.wait_recv()
            for k, (end, rows) in enumerate(((r_end_up, upper), (r_end_down, lower))):
                end.wait_recv()
                product = cube[it, 0, rows] + (x_ended[it, k] + x_chain[it, 2 + k])
                value = block[it, 0, rows]
                if it == 0:
                    f = factor[0:1, 0:1]
                    new = (1.5 * f) * value - (0.5 * f) * product
                else:
                    new = 1.5 * value - 0.5 * product
                if it == ITERS - 1:
                    o_ref[rows] = new
                else:
                    block[it + 1, 0, rows] = new

        sy, sz = {}, {}
        if it == 0:
            for k, peer in enumerate(y_peers, 1):
                sy[k] = copy(sums_y.at[0], sums_y.at[k], s_send.at[k], s_recv.at[k], peer)
            for k, peer in enumerate(z_peers, 1):
                sz[k] = copy(sums_z.at[0], sums_z.at[k], s_send.at[8 + k], s_recv.at[8 + k], peer)

        def sums1():
            tile = jnp.zeros((8, 128), F32)
            for v in (block[it, 0], panel[it, 1], panel[it, 2], panel[it, 3]):
                v = v.reshape(ROWS // 8, 8, STRIP)
                tile = tile + jnp.sum(v * v, axis=0)
            sums_y[0] = tile
            for made in sy.values():
                go(made)

        def sums2():
            for made in sy.values():
                made.wait_recv()
            sums_z[0] = jnp.sum(sums_y[...], axis=0)
            for made in sz.values():
                go(made)

        def sums3():
            for made in sz.values():
                made.wait_recv()
            total = jnp.sum(jnp.sum(sums_z[...], axis=0), keepdims=True)
            factor[...] = jnp.broadcast_to(jnp.sqrt(N / total), factor.shape)

        work = dict(
            own=own, zd=zd, zu=zu, put=put, xfu=xfu, xfd=xfd, xnear=xnear, xlast=xlast, mul=mul,
            s1=s1, s2=s2, s3=s3, s6=s6, rc=rc, rn=rn, re=re, fin=fin,
            sums1=sums1, sums2=sums2, sums3=sums3,
        )
        for name, *args in ORDER[it]:
            with jax.named_scope("_".join([f"i{it}", name, *map(str, args)])):
                work[name](*args)

    for it in range(ITERS):
        iteration(it)
    for made in pending:
        made.wait_send()


def shards(matrix):
    dma = pltpu.SemaphoreType.DMA
    wide = NX * STRIP
    widths = [n * STRIP for _, n in LANES]

    def per_set(*shape):
        return [pltpu.VMEM((ITERS, NZ, *shape, width), F32) for width in widths]

    return pl.pallas_call(
        kernel,
        out_shape=jax.ShapeDtypeStruct((ROWS, STRIP), F32),
        in_specs=[pl.BlockSpec(memory_space=pltpu.VMEM)],
        out_specs=pl.BlockSpec(memory_space=pltpu.VMEM),
        scratch_shapes=[
            pltpu.VMEM((ITERS, NZ, ROWS, STRIP), F32),
            pltpu.VMEM((ITERS, NX, ROWS, STRIP), F32),
            pltpu.VMEM((ROWS, NZ * STRIP), BF),
            pltpu.VMEM((ROWS, NZ * STRIP), BF),
            pltpu.VMEM((ROWS, wide), BF),
            pltpu.VMEM((ROWS, wide), BF),
            pltpu.VMEM((NZ * STRIP, wide), BF),
            pltpu.VMEM((NZ * STRIP, wide), BF),
            *per_set(NC, SROWS),
            *per_set(SROWS),
            *per_set(SROWS),
            *per_set(SROWS),
            *per_set(SROWS),
            *per_set(SROWS),
            *per_set(NC, SROWS),
            pltpu.VMEM((ITERS, NX, ROWS, STRIP), F32),
            pltpu.VMEM((ITERS, 4, HALF, STRIP), F32),
            pltpu.VMEM((ITERS, 2, HALF, STRIP), F32),
            pltpu.VMEM((8, 128), F32),
            pltpu.VMEM((NY * NC, 8, 128), F32),
            pltpu.VMEM((NZ, 8, 128), F32),
            dma((ITERS, NZ, 2)),
            dma((ITERS, NZ, 2)),
            dma((ITERS, 12)),
            dma((ITERS, 12)),
            dma((ITERS, len(GROUPS), len(SETS), 6)),
            dma((ITERS, len(GROUPS), len(SETS), 6)),
            dma((NY * NC + NZ,)),
            dma((NY * NC + NZ,)),
        ],
        compiler_params=pltpu.CompilerParams(
            collective_id=0, has_side_effects=True, vmem_limit_bytes=56 * 1024 * 1024
        ),
    )(matrix)


def solution(mesh):
    grid = Mesh(mesh.devices.reshape(NY, NC, NX, NZ), ("y", "c", "x", "z"))
    spec = P(("y", "c"), ("x", "z"))
    return jax.shard_map(shards, mesh=grid, in_specs=(spec,), out_specs=spec, check_vma=False)
```

time: 326 us -> 111 us (0.34)
  waiting for transfers between devices: 127 us -> 0 us
  blocking collectives: 120 us -> 0 us
  Pallas kernels: 0 us -> 109 us
  matrix products: 42.2 us -> 0 us
  starting transfers between devices: 15 us -> 0 us
  between operations: 14.2 us -> 0.01 us
  local copies, waits for them, and re-layouts: 6.33 us -> 1.67 us
    pallas_call x0 -> x1, Pallas kernels: none -> 109 us  [shards(): pl.pallas_call(kernel, out_shape=jax.ShapeDtypeStruct((ROWS, STRIP), F32)...]
    all_gather x2 -> x0, waiting for transfers between devices: 100 us -> none  [shards(): rows_panel = lax.all_gather(source, COL, axis=1, tiled=True)]
    all_to_all x2 -> x0, blocking collectives: 61.4 us -> none  [sent_to_all(): return lax.all_to_all(copies, axis, split_axis=0, concat_axis=0, tiled=True)]
    psum x4 -> x0, blocking collectives: 58.5 us -> none  [by_axis(): array = lax.psum(array, axis)]
    dot_general x4 -> x0, matrix products: 42.2 us -> none  [the longest x2 24.8 us: shards(): jnp.dot(rows_panel, cols_panel, preferred_element_type=jnp.float32, preci...]
    all_to_all x2 -> x0, waiting for transfers between devices: 26.1 us -> none  [sent_to_all(): return lax.all_to_all(copies, axis, split_axis=0, concat_axis=0, tiled=True)]
    all_to_all x2 -> x0, starting transfers between devices: 15 us -> none  [sent_to_all(): return lax.all_to_all(copies, axis, split_axis=0, concat_axis=0, tiled=True)]
    broadcast_in_dim x4 -> x0, local copies, waits for them, and re-layouts: 4.28 us -> none  [sent_to_all(): copies = jnp.broadcast_to(array, (lax.axis_size(axis), *array.shape))]
  transfers between devices with their start and end apart: 4 -> 0, of which waited for: 3 -> 0; matrix products, arithmetic and copies ran while one was open for 1% -> 0% of each run, Pallas kernels for 0% -> 0%
where the time goes in v2:
time: 111 us
  Pallas kernels  109 us (98%)
  local copies, waits for them, and re-layouts  1.67 us (2%)
    pallas_call x1, Pallas kernels, shards(): pl.pallas_call(kernel, out_shape=jax.ShapeDtypeStruct((ROWS, STRIP), F32)...  109 us

profile of v2, /device:TPU:1, one launch (start us, length us, event | category | flops | bytes accessed | tf_op | source)
XLA Modules:
  0.0 110.8 jit_solution(42127587091987093)
XLA Ops:
  0.0 109.1 %shard_map.17 = f32[512,128]{1,0:T(8,128)} custom-call(f32[512,128]{1,0:T(8,128)} %m_ref.1), custom_call_target="tpu_custom_call" | custom-call | tf_op jit(solution)/shard_map/pallas_call | solution.py:370
  109.1 1.7 %copy.3 = f32[512,128]{1,0:T(8,128)} copy(f32[512,128]{1,0:T(8,128)} %shard_map.17) | data formatting | bytes 524288

commit v3 on v2

v3 whole, which is shorter than its diff:
```python
import jax
import jax.numpy as jnp
from jax import lax
from jax.experimental import pallas as pl
from jax.experimental.pallas import tpu as pltpu
from jax.sharding import Mesh
from jax.sharding import PartitionSpec as P

N = 4096
ITERS = 2
NY, NC, NX, NZ = 4, 2, 4, 8
ROWS = N // (NY * NC)
STRIP = N // (NX * NZ)
HALF = ROWS // 2
PIECES = 4
PIECE = ROWS // PIECES
SROWS = STRIP // NC
SHALF = SROWS // 2
SQUARTER = SROWS // 4
GROUPS = ((0, 1), (1, 2), (3, 2), (5, 2), (7, 1))
SETS = ((2,), (1, 3), (0,))
LANES = ((0, 1), (1, 2), (3, 1))
BF = jnp.bfloat16
F32 = jnp.float32
THREE_STEPS = 12
ORDER = (
    (
        ("oxu", 2), ("oxd", 1), ("ozu", 2), ("oxd", 3), ("ozu", 1), ("ozd", 0), ("put", 0), ("oxu", 0), ("ozd", 2),
        ("ozu", 0), ("ozd", 1), ("oxu", 1), ("ozu", 3), ("ozd", 3), ("oxd", 2), ("oxu", 3), ("oxd", 0),
        ("mul", 0, 2), ("s1", 0, 2), ("zd", 1, 0, 0), ("zu", 2, 2, 0), ("s2", 0, 2), ("zu", 2, 1, 0),
        ("zd", 1, 2, 0), ("xfu", 0), ("xfd", 3), ("zd", 1, 1, 0), ("zu", 2, 0, 0), ("xfd", 2), ("xfu", 1),
        ("s3", 0, 2), ("zd", 1, 3, 0), ("put", 1), ("zu", 2, 3, 0), ("put", 2), ("mul", 1, 2), ("xnear",),
        ("mul", 1, 1), ("mul", 0, 1), ("zu", 4, 2, 0), ("zd", 3, 0, 0), ("s1", 1, 2), ("s4", 0, 2), ("s1", 1, 1),
        ("s1", 0, 1), ("zd", 3, 2, 0), ("zu", 4, 1, 0), ("xlast",), ("mul", 1, 0), ("mul", 0, 0), ("sums1",),
        ("zu", 4, 0, 0), ("zd", 3, 1, 0), ("s1", 1, 0), ("s2", 1, 2), ("s1", 0, 0), ("zd", 3, 3, 0),
        ("zu", 4, 3, 0), ("put", 4), ("put", 3), ("mul", 2), ("s2", 1, 1), ("s2", 0, 1), ("zu", 6, 2, 0),
        ("zd", 5, 0, 0), ("s1", 2, 0), ("sums2",), ("s2", 1, 0), ("s1", 2, 1), ("s1", 2, 2), ("s3", 1, 2),
        ("zd", 5, 2, 0), ("zu", 6, 1, 0), ("s2", 0, 0), ("zu", 6, 0, 0), ("s3", 1, 1), ("zd", 5, 1, 0),
        ("s3", 0, 1), ("s2", 2, 0), ("s3", 1, 0), ("zd", 5, 3, 0), ("put", 5), ("zu", 6, 3, 0), ("put", 6),
        ("mul", 3), ("s2", 2, 1), ("s2", 2, 2), ("s4", 1, 2), ("s3", 0, 0), ("s1", 3, 0), ("s4", 1, 1),
        ("s1", 3, 1), ("s1", 3, 2), ("s4", 0, 1), ("s3", 2, 0), ("sums3",), ("s4", 1, 0), ("put", 7), ("mul", 4),
        ("s3", 2, 1), ("s3", 2, 2), ("s4", 0, 0), ("s2", 3, 0), ("s1", 4, 0), ("s1", 4, 1), ("s1", 4, 2),
        ("s2", 3, 1), ("s6", 0), ("s4", 2, 0), ("s6", 1), ("s4", 2, 1), ("s2", 3, 2), ("s6", 2, 0), ("s3", 3, 0),
        ("s4", 2, 2), ("s2", 4, 0), ("s6", 2, 1), ("s2", 4, 1), ("s2", 4, 2), ("s6", 2, 2), ("s3", 3, 1),
        ("s3", 3, 2), ("s4", 3, 0), ("s3", 4, 0), ("s6", 3, 0), ("s6", 4, 0), ("rc", 0), ("s3", 4, 2), ("s3", 4, 1),
        ("rc", 1), ("s4", 3, 1), ("s4", 3, 2), ("s6", 3, 1), ("s6", 4, 1), ("rn", 1), ("rn", 0), ("s6", 3, 2),
        ("s6", 4, 2), ("re", 0), ("re", 1), ("fin", 0), ("fin", 1),
    ),
    (
        ("oxd", 2), ("ozu", 2), ("oxu", 2), ("oxu", 0), ("ozu", 0), ("oxd", 0), ("ozd", 2), ("ozd", 0), ("ozd", 1),
        ("oxd", 3), ("oxu", 1), ("ozd", 3), ("ozu", 1), ("oxd", 1), ("put", 0), ("mul", 0, 2), ("oxu", 3),
        ("ozu", 3), ("s1", 0, 2), ("zd", 1, 2, 0), ("zu", 2, 2, 0), ("xfd", 2), ("zd", 1, 0, 0), ("zu", 2, 0, 0),
        ("xfu", 0), ("s2", 0, 2), ("zd", 1, 1, 0), ("zu", 2, 1, 0), ("xfd", 3), ("xfu", 1), ("zd", 1, 3, 0),
        ("put", 1), ("zu", 2, 3, 0), ("put", 2), ("mul", 1, 2), ("xnear",), ("mul", 0, 1), ("s3", 0, 2),
        ("mul", 1, 1), ("zd", 3, 2, 0), ("zu", 4, 2, 0), ("s1", 1, 2), ("s1", 0, 1), ("zd", 3, 0, 0),
        ("zu", 4, 0, 0), ("s1", 1, 1), ("xlast",), ("mul", 0, 0), ("mul", 1, 0), ("s4", 0, 2), ("zu", 4, 1, 0),
        ("zd", 3, 1, 0), ("s1", 0, 0), ("s2", 1, 2), ("s1", 1, 0), ("s2", 0, 1), ("zu", 4, 3, 0), ("put", 4),
        ("zd", 3, 3, 0), ("put", 3), ("mul", 2), ("s2", 1, 1), ("zu", 6, 2, 0), ("zd", 5, 2, 0), ("s2", 0, 0),
        ("s1", 2, 0), ("s1", 2, 1), ("s1", 2, 2), ("s3", 1, 2), ("zu", 6, 0, 0), ("s2", 1, 0), ("zd", 5, 0, 0),
        ("s3", 0, 1), ("zu", 6, 1, 0), ("s3", 1, 1), ("zd", 5, 1, 0), ("s3", 0, 0), ("s2", 2, 0), ("zd", 5, 3, 0),
        ("put", 5), ("zu", 6, 3, 0), ("put", 6), ("mul", 3), ("s2", 2, 1), ("s2", 2, 2), ("s4", 1, 2), ("s3", 1, 0),
        ("s4", 0, 1), ("s1", 3, 0), ("s1", 3, 1), ("s4", 1, 1), ("s1", 3, 2), ("s4", 0, 0), ("s3", 2, 0),
        ("put", 7), ("mul", 4), ("s3", 2, 1), ("s6", 0), ("s3", 2, 2), ("s4", 1, 0), ("s2", 3, 0), ("s1", 4, 0),
        ("s1", 4, 1), ("s1", 4, 2), ("s2", 3, 1), ("s2", 3, 2), ("s6", 1), ("s4", 2, 0), ("s4", 2, 1), ("s4", 2, 2),
        ("s3", 3, 0), ("s2", 4, 0), ("s6", 2, 0), ("s6", 2, 2), ("s2", 4, 1), ("s6", 2, 1), ("s3", 3, 1),
        ("s2", 4, 2), ("s3", 3, 2), ("s4", 3, 0), ("s3", 4, 0), ("s6", 3, 0), ("s6", 4, 0), ("rc", 0), ("rc", 1),
        ("s3", 4, 1), ("s4", 3, 1), ("s3", 4, 2), ("s4", 3, 2), ("s6", 3, 1), ("s6", 4, 1), ("rn", 0), ("rn", 1),
        ("s6", 3, 2), ("s6", 4, 2), ("re", 0), ("re", 1), ("fin", 0), ("fin", 1),
    ),
)


def split(value):
    high = value.astype(BF)
    return high, (value - high.astype(F32)).astype(BF)


def three(dim, a, b):
    a = jnp.concatenate([a[0], a[1], a[0]], axis=dim)
    b = jnp.concatenate([b[0], b[0], b[1]], axis=0)
    return lax.dot_general(a, b, (((dim,), (0,)), ((), ())), preferred_element_type=F32)


def lanes_of(s):
    first, n = LANES[s]
    return slice(first * STRIP, (first + n) * STRIP)


def kernel(m_ref, o_ref, block, panel, block_hi, block_lo, panel_hi, panel_lo, square_hi, square_lo, *refs):
    ns = len(SETS)
    part, from_core, mine, first_in, ours, second_in, square = (refs[k * ns : (k + 1) * ns] for k in range(7))
    (
        cube, x_chain, x_ended, factor, sums_y, sums_z, out,
        z_send, z_recv, x_send, x_recv, r_send, r_recv, g_send, g_recv, s_send, s_recv, local_sem,
    ) = refs[7 * ns :]
    y, c, x, z = (lax.axis_index(name) for name in ("y", "c", "x", "z"))

    def turn(name, here, by, size):
        return {name: lax.rem(here + by, size)}

    up_z, down_z = turn("z", z, 1, NZ), turn("z", z, NZ - 1, NZ)
    up_x, down_x = turn("x", x, 1, NX), turn("x", x, NX - 1, NX)
    odd = lax.rem(y, 2)
    y_near, y_far = turn("y", y, NY + 1 - 2 * odd, NY), turn("y", y, NY - 1 + 2 * odd, NY)
    other_core = {"c": 1 - c}
    z_peers = [turn("z", z, d, NZ) for d in range(1, NZ)]
    y_peers = [{"y": lax.rem(y + d, NY), "c": lax.rem(c + e, NC)} for d in range(NY) for e in range(NC)][1:]

    barrier = pltpu.get_barrier_semaphore()
    peers = [up_x, down_x, *z_peers, *y_peers]
    for peer in peers:
        pl.semaphore_signal(barrier, inc=1, device_id=peer, device_id_type=pl.DeviceIdType.MESH)
    fetch = pltpu.make_async_copy(m_ref, block.at[0, 0], local_sem.at[0])
    fetch.start()
    fetch.wait()
    pl.semaphore_wait(barrier, len(peers))

    def copy(src, dst, send, recv, peer):
        return pltpu.make_async_remote_copy(
            src_ref=src, dst_ref=dst, send_sem=send, recv_sem=recv,
            device_id=peer, device_id_type=pl.DeviceIdType.MESH,
        )

    def go(made):
        made.start()

    def all_sent(ref, sem):
        copy(ref, ref, sem, local_sem.at[5], up_x).wait_send()

    low, high = pl.ds(0, SHALF), pl.ds(SHALF, SHALF)
    gray, top = lax.rem(lax.div(y + 1, 2), 2), lax.div(y, 2)

    def sub(half, which):
        return pl.ds(pl.multiple_of(half * SHALF + which * SQUARTER, SQUARTER), SQUARTER)

    stored = []

    def iteration(it):
        block_i, panel_i, cube_i = block.at[it], panel.at[it], cube.at[it]

        def piece_of(q):
            return pl.ds(q * PIECE, PIECE)

        def z_copy(src, dst, q, peer):
            return copy(
                block_i.at[src, piece_of(q)], block_i.at[dst, piece_of(q)],
                z_send.at[it], z_recv.at[it, dst, q], peer,
            )

        every_piece, upper_pieces, lower_pieces = range(PIECES), (0, 1), (2, 3)
        ups = {(p, q): z_copy(max(p - 2, 0), p, q, up_z) for p in (2, 4, 6) for q in every_piece}
        downs = {(p, q): z_copy(max(p - 2, 0), p, q, down_z) for p in (1, 3, 5) for q in every_piece}
        ups.update({(8, q): z_copy(6, 7, q, up_z) for q in upper_pieces})
        downs.update({(7, q): z_copy(5, 7, q, down_z) for q in lower_pieces})

        def x_copy(src, dst, q, peer):
            return copy(
                src.at[piece_of(q)], panel_i.at[dst, piece_of(q)], x_send.at[it], x_recv.at[it, dst, q], peer
            )

        x_up = [x_copy(block_i.at[0], 3, q, up_x) for q in every_piece]
        x_down = [x_copy(block_i.at[0], 1, q, down_x) for q in every_piece]
        x_far = [x_copy(panel_i.at[3], 2, q, up_x) for q in upper_pieces]
        x_far += [x_copy(panel_i.at[1], 2, q, down_x) for q in lower_pieces]

        def put_panel(slot, value):
            at = {2: 0, 1: 1, 3: 2, 0: 3}[slot]
            columns = slice(at * STRIP, (at + 1) * STRIP)
            panel_hi[:, columns], panel_lo[:, columns] = split(value)

        def ozu(q):
            go(ups[2, q])

        def ozd(q):
            go(downs[1, q])

        def oxu(q):
            go(x_up[q])

        def oxd(q):
            go(x_down[q])

        def zd(pos, piece, _):
            downs[pos, piece].wait_recv()
            if (pos + 2, piece) in downs:
                go(downs[pos + 2, piece])

        def zu(pos, piece, _):
            ups[pos, piece].wait_recv()
            if (pos + 2, piece) in ups:
                go(ups[pos + 2, piece])

        def put(pos):
            if pos == 7:
                for q in upper_pieces:
                    ups[8, q].wait_recv()
                for q in lower_pieces:
                    downs[7, q].wait_recv()
            columns = slice(pos * STRIP, (pos + 1) * STRIP)
            value = block[it, pos]
            block_hi[:, columns], block_lo[:, columns] = split(value)
            if pos == 0:
                put_panel(0, value)

        def xfu(q):
            x_up[q].wait_recv()
            go(x_far[q])

        def xfd(q):
            x_down[q].wait_recv()
            go(x_far[q])

        def xnear():
            for q in lower_pieces:
                x_up[q].wait_recv()
            for q in upper_pieces:
                x_down[q].wait_recv()
            put_panel(3, panel[it, 3])
            put_panel(1, panel[it, 1])

        def xlast():
            for q in every_piece:
                x_far[q].wait_recv()
            put_panel(2, panel[it, 2])

        def unit(g, s):
            run = pl.ds(*GROUPS[g])
            every = slice(None)

            three_steps = g * ns + s < THREE_STEPS

            def made(k, src, dst, peer):
                to = 0 if k in (0, 5) else 1 if not three_steps else 2 + {1: 0, 2: 0, 3: 1, 4: 1, 6: 2, 7: 2}[k]
                return copy(src, dst, g_send.at[it, s, to], g_recv.at[it, g, s, k], peer)

            def rows(ref, which):
                return ref[s].at[it, run, which]

            sums = square[s].at[it, run, c]
            cs = dict(
                core=made(0, part[s].at[it, run, 1 - c], from_core[s].at[it, run], other_core),
                join=made(5, sums, sums, other_core),
            )
            if three_steps:
                one, two = (sub(0, 1 - gray), sub(1, 1 - top)), (sub(0, gray), sub(1, top))
                low_sums, high_sums = square[s].at[it, run, c, two[0]], square[s].at[it, run, c, two[1]]
                cs["low_three"] = made(6, low_sums, low_sums, y_near)
                cs["high_three"] = made(7, high_sums, high_sums, y_far)
            else:
                one = two = (low, high)
            cs["low_one"] = made(1, rows(mine, one[0]), rows(first_in, one[0]), y_near)
            cs["high_one"] = made(2, rows(mine, one[1]), rows(first_in, one[1]), y_far)
            cs["low_two"] = made(3, rows(ours, two[0]), rows(second_in, two[0]), y_far)
            cs["high_two"] = made(4, rows(ours, two[1]), rows(second_in, two[1]), y_near)
            cs["kept"] = two
            return cs

        units = {(g, s): unit(g, s) for g in range(len(GROUPS)) for s in range(ns)}

        def strips(g):
            first, n = GROUPS[g]
            return range(first, first + n)

        def factors(g):
            first, n = GROUPS[g]
            columns = slice(first * STRIP, (first + n) * STRIP)
            return block_hi[:, columns], block_lo[:, columns]

        def mul(g, *which):
            first, n = GROUPS[g]
            columns = lanes_of(which[0]) if which else slice(0, NX * STRIP)
            got = three(0, factors(g), (panel_hi[:, columns], panel_lo[:, columns]))
            for s in which or range(ns):
                piece = got if which else got[:, lanes_of(s)]
                part[s][it, first : first + n] = piece.reshape(n, NC, SROWS, piece.shape[1])
                go(units[g, s]["core"])

        def s1(g, s):
            cs = units[g, s]
            cs["core"].wait_recv()
            for p in strips(g):
                mine[s][it, p] = part[s][it, p, c] + from_core[s][it, p]
            go(cs["low_one"])
            go(cs["high_one"])

        def s2(g, s):
            cs = units[g, s]
            for half, kept in zip(("low", "high"), cs["kept"]):
                cs[half + "_one"].wait_recv()
                for p in strips(g):
                    ours[s][it, p, kept] = mine[s][it, p, kept] + first_in[s][it, p, kept]
                go(cs[half + "_two"])

        def s3(g, s):
            cs = units[g, s]
            for half, kept in zip(("low", "high"), cs["kept"]):
                cs[half + "_two"].wait_recv()
                for p in strips(g):
                    square[s][it, p, c, kept] = ours[s][it, p, kept] + second_in[s][it, p, kept]
                if half + "_three" in cs:
                    go(cs[half + "_three"])
            if "low_three" not in cs:
                go(cs["join"])

        def s4(g, s):
            cs = units[g, s]
            cs["low_three"].wait_recv()
            cs["high_three"].wait_recv()
            go(cs["join"])

        def s6(g, *which):
            first, n = GROUPS[g]
            rows = slice(first * STRIP, (first + n) * STRIP)
            todo = which or range(ns)
            for s in todo:
                units[g, s]["join"].wait_recv()
                value = square[s][it, first : first + n]
                value = value.reshape(n * STRIP, value.shape[-1])
                if it == 0:
                    f = factor[0:1, 0:1]
                    value = value * (f * f)
                square_hi[rows, lanes_of(s)], square_lo[rows, lanes_of(s)] = split(value)
            columns = lanes_of(which[0]) if which else slice(0, NX * STRIP)
            got = three(1, factors(g), (square_hi[rows, columns], square_lo[rows, columns]))
            for k, slot in enumerate([slot for s in todo for slot in SETS[s]]):
                piece = got[:, k * STRIP : (k + 1) * STRIP]
                if first == 0:
                    cube[it, slot] = piece
                else:
                    cube[it, slot] += piece

        def reduce_copies(r):
            upper, lower = pl.ds(r * PIECE, PIECE), pl.ds(HALF + r * PIECE, PIECE)

            def made(k, slot, rows, dst, peer):
                return copy(cube_i.at[slot, rows], dst, r_send.at[it], r_recv.at[it, r, k], peer)

            return dict(
                chain_up=made(0, 2, upper, x_chain.at[it, r, 0], up_x),
                chain_down=made(1, 2, lower, x_chain.at[it, r, 1], down_x),
                near_down=made(2, 3, upper, x_chain.at[it, r, 2], down_x),
                near_up=made(3, 1, lower, x_chain.at[it, r, 3], up_x),
                end_up=made(4, 1, upper, x_ended.at[it, r, 0], up_x),
                end_down=made(5, 3, lower, x_ended.at[it, r, 1], down_x),
                rows=(upper, lower),
            )

        reduces = [reduce_copies(r) for r in range(2)]

        def rc(r):
            go(reduces[r]["chain_up"])
            go(reduces[r]["chain_down"])

        def rn(r):
            go(reduces[r]["near_up"])
            go(reduces[r]["near_down"])

        def re(r):
            cs = reduces[r]
            for k, (slot, way) in enumerate(((1, "up"), (3, "down"))):
                cs["chain_" + way].wait_recv()
                cube[it, slot, cs["rows"][k]] += x_chain[it, r, k]
                go(cs["end_" + way])

        def fin(r):
            cs = reduces[r]
            cs["near_down"].wait_recv()
            cs["near_up"].wait_recv()
            for k, way in enumerate(("up", "down")):
                cs["end_" + way].wait_recv()
                rows = cs["rows"][k]
                product = cube[it, 0, rows] + (x_ended[it, r, k] + x_chain[it, r, 2 + k])
                value = block[it, 0, rows]
                if it == 0:
                    f = factor[0:1, 0:1]
                    new = (1.5 * f) * value - (0.5 * f) * product
                else:
                    new = 1.5 * value - 0.5 * product
                if it == ITERS - 1:
                    out[rows] = new
                    store = pltpu.make_async_copy(out.at[rows], o_ref.at[rows], local_sem.at[1 + 2 * r + k])
                    store.start()
                    stored.append(store)
                else:
                    block[it + 1, 0, rows] = new

        sy, sz = {}, {}
        if it == 0:
            for k, peer in enumerate(y_peers, 1):
                sy[k] = copy(sums_y.at[0], sums_y.at[k], s_send.at[0], s_recv.at[k], peer)
            for k, peer in enumerate(z_peers, 1):
                sz[k] = copy(sums_z.at[0], sums_z.at[k], s_send.at[1], s_recv.at[8 + k], peer)

        def sums1():
            tile = jnp.zeros((8, 128), F32)
            for v in (block[it, 0], panel[it, 1], panel[it, 2], panel[it, 3]):
                v = v.reshape(ROWS // 8, 8, STRIP)
                tile = tile + jnp.sum(v * v, axis=0)
            sums_y[0] = tile
            for made in sy.values():
                go(made)

        def sums2():
            for made in sy.values():
                made.wait_recv()
            sums_z[0] = jnp.sum(sums_y[...], axis=0)
            for made in sz.values():
                go(made)

        def sums3():
            for made in sz.values():
                made.wait_recv()
            total = jnp.sum(jnp.sum(sums_z[...], axis=0), keepdims=True)
            factor[...] = jnp.broadcast_to(jnp.sqrt(N / total), factor.shape)

        work = dict(
            ozu=ozu, ozd=ozd, oxu=oxu, oxd=oxd, zd=zd, zu=zu, put=put, xfu=xfu, xfd=xfd, xnear=xnear, xlast=xlast, mul=mul,
            s1=s1, s2=s2, s3=s3, s4=s4, s6=s6, rc=rc, rn=rn, re=re, fin=fin,
            sums1=sums1, sums2=sums2, sums3=sums3,
        )
        for name, *args in ORDER[it]:
            with jax.named_scope("_".join([f"i{it}", name, *map(str, args)])):
                work[name](*args)

    for it in range(ITERS):
        iteration(it)
    for it in range(ITERS):
        all_sent(block.at[it, pl.ds(0, NZ - 1)], z_send.at[it])
        all_sent(panel.at[it, pl.ds(0, NX - 1)], x_send.at[it])
        all_sent(cube.at[it, pl.ds(0, NX - 1)], r_send.at[it])
        for s in range(ns):
            slow = sum(n for g, (_, n) in enumerate(GROUPS) if g * ns + s < THREE_STEPS)
            all_sent(square[s].at[it], g_send.at[it, s, 0])
            if slow < NZ:
                all_sent(square[s].at[it, pl.ds(0, NZ - slow)], g_send.at[it, s, 1])
            for k in range(3 if slow else 0):
                all_sent(mine[s].at[it, pl.ds(0, slow), low], g_send.at[it, s, 2 + k])
    all_sent(sums_y.at[pl.ds(1, NY * NC - 1)], s_send.at[0])
    all_sent(sums_z.at[pl.ds(1, NZ - 1)], s_send.at[1])
    for store in stored:
        store.wait()


def shards(matrix):
    dma = pltpu.SemaphoreType.DMA
    wide = NX * STRIP
    widths = [n * STRIP for _, n in LANES]

    def per_set(*shape):
        return [pltpu.VMEM((ITERS, NZ, *shape, width), F32) for width in widths]

    return pl.pallas_call(
        kernel,
        out_shape=jax.ShapeDtypeStruct((ROWS, STRIP), F32),
        in_specs=[pl.BlockSpec(memory_space=pltpu.HBM)],
        out_specs=pl.BlockSpec(memory_space=pltpu.HBM),
        scratch_shapes=[
            pltpu.VMEM((ITERS, NZ, ROWS, STRIP), F32),
            pltpu.VMEM((ITERS, NX, ROWS, STRIP), F32),
            pltpu.VMEM((ROWS, NZ * STRIP), BF),
            pltpu.VMEM((ROWS, NZ * STRIP), BF),
            pltpu.VMEM((ROWS, wide), BF),
            pltpu.VMEM((ROWS, wide), BF),
            pltpu.VMEM((NZ * STRIP, wide), BF),
            pltpu.VMEM((NZ * STRIP, wide), BF),
            *per_set(NC, SROWS),
            *per_set(SROWS),
            *per_set(SROWS),
            *per_set(SROWS),
            *per_set(SROWS),
            *per_set(SROWS),
            *per_set(NC, SROWS),
            pltpu.VMEM((ITERS, NX, ROWS, STRIP), F32),
            pltpu.VMEM((ITERS, 2, 4, PIECE, STRIP), F32),
            pltpu.VMEM((ITERS, 2, 2, PIECE, STRIP), F32),
            pltpu.VMEM((8, 128), F32),
            pltpu.VMEM((NY * NC, 8, 128), F32),
            pltpu.VMEM((NZ, 8, 128), F32),
            pltpu.VMEM((ROWS, STRIP), F32),
            dma((ITERS,)),
            dma((ITERS, NZ, PIECES)),
            dma((ITERS,)),
            dma((ITERS, NX, PIECES)),
            dma((ITERS,)),
            dma((ITERS, 2, 6)),
            dma((ITERS, len(SETS), 5)),
            dma((ITERS, len(GROUPS), len(SETS), 8)),
            dma((2,)),
            dma((NY * NC + NZ,)),
            dma((6,)),
        ],
        compiler_params=pltpu.CompilerParams(
            collective_id=0, has_side_effects=True, vmem_limit_bytes=56 * 1024 * 1024
        ),
    )(matrix)


def solution(mesh):
    grid = Mesh(mesh.devices.reshape(NY, NC, NX, NZ), ("y", "c", "x", "z"))
    spec = P(("y", "c"), ("x", "z"))
    return jax.shard_map(shards, mesh=grid, in_specs=(spec,), out_specs=spec, check_vma=False)
```

time: 111 us -> 106 us (0.955)
  Pallas kernels: 109 us -> 104 us
    pallas_call x1, Pallas kernels: 109 us -> 104 us  [shards(): pl.pallas_call(kernel, out_shape=jax.ShapeDtypeStruct((ROWS, STRIP), F32)...]
where the time goes in v3:
time: 106 us
  Pallas kernels  104 us (98%)
  local copies, waits for them, and re-layouts  1.67 us (2%)
    pallas_call x1, Pallas kernels, shards(): pl.pallas_call(kernel, out_shape=jax.ShapeDtypeStruct((ROWS, STRIP), F32)...  104 us

profile of v3, /device:TPU:1, one launch (start us, length us, event | category | flops | bytes accessed | tf_op | source)
XLA Modules:
  0.0 105.7 jit_solution(6049042805606155799)
XLA Ops:
  0.0 104.0 %shard_map.17 = f32[512,128]{1,0:T(8,128)} custom-call(f32[512,128]{1,0:T(8,128)} %m_ref.1), custom_call_target="tpu_custom_call" | custom-call | tf_op jit(solution)/shard_map/pallas_call | solution.py:452
  104.0 1.7 %copy.3 = f32[512,128]{1,0:T(8,128)} copy(f32[512,128]{1,0:T(8,128)} %shard_map.17) | data formatting | bytes 524288

commit v4 on v3

v4 whole, which is shorter than its diff:
```python
import jax
import jax.numpy as jnp
from jax import lax
from jax.experimental import pallas as pl
from jax.experimental.pallas import tpu as pltpu
from jax.sharding import Mesh
from jax.sharding import PartitionSpec as P

N = 4096
ITERS = 2
NY, NC, NX, NZ = 4, 2, 4, 8
ROWS = N // (NY * NC)
STRIP = N // (NX * NZ)
HALF = ROWS // 2
PIECES = 4
PIECE = ROWS // PIECES
SROWS = STRIP // NC
SHALF = SROWS // 2
SQUARTER = SROWS // 4
GROUPS = ((0, 1), (1, 2), (3, 2), (5, 2), (7, 1))
SETS = ((2,), (1, 3), (0,))
LANES = ((0, 1), (1, 2), (3, 1))
BF = jnp.bfloat16
F32 = jnp.float32
MERGED = (0,)
THREE_STEPS = 12
ORDER = (
    (
        ("own", 0), ("put", 0), ("mul", 0, 2), ("own", 1), ("s1", 0, 2), ("zz", 0, 0), ("xf", 0), ("s2", 0, 2),
        ("zz", 0, 1), ("zz", 0, 2), ("xf", 1), ("s3", 0, 2), ("zz", 0, 3), ("put", 1), ("put", 2), ("mul", 1, 2),
        ("xnear",), ("mul", 1, 1), ("mul", 0, 1), ("zz", 1, 0), ("s1", 1, 2), ("s4", 0, 2), ("s1", 1, 1),
        ("zz", 1, 1), ("s1", 0, 1), ("xlast",), ("sums1",), ("mul", 0, 0), ("mul", 1, 0), ("zz", 1, 2),
        ("s1", 0, 0), ("s2", 1, 2), ("s1", 1, 0), ("zz", 1, 3), ("put", 3), ("put", 4), ("mul", 2), ("s2", 1, 1),
        ("s2", 0, 1), ("zz", 2, 0), ("sums2",), ("s2", 0, 0), ("s1", 2, 0), ("s1", 2, 1), ("s1", 2, 2),
        ("s3", 1, 2), ("zz", 2, 1), ("s2", 1, 0), ("zz", 2, 2), ("s3", 1, 1), ("s3", 0, 1), ("s3", 0, 0),
        ("s2", 2, 0), ("zz", 2, 3), ("put", 6), ("put", 5), ("mul", 3), ("s2", 2, 1), ("s2", 2, 2), ("s4", 1, 2),
        ("s3", 1, 0), ("s1", 3, 0), ("s4", 1, 1), ("sums3",), ("s4", 0, 1), ("s1", 3, 1), ("s1", 3, 2),
        ("s4", 0, 0), ("put", 7), ("mul", 4), ("s3", 2, 0), ("s6", 0), ("s3", 2, 1), ("s6", 1, 1), ("s6", 1, 2),
        ("s2", 3, 0), ("s4", 1, 0), ("s1", 4, 0), ("s1", 4, 2), ("s3", 2, 2), ("s1", 4, 1), ("s2", 3, 1),
        ("s2", 3, 2), ("s6", 1, 0), ("s4", 2, 0), ("s4", 2, 1), ("s3", 3, 0), ("s6", 2, 0), ("s2", 4, 0),
        ("s2", 4, 2), ("s6", 2, 1), ("s4", 2, 2), ("s2", 4, 1), ("s3", 3, 1), ("s6", 2, 2), ("s3", 3, 2),
        ("s4", 3, 0), ("s3", 4, 0), ("s3", 4, 2), ("s6", 3, 0), ("s6", 4, 0), ("rc", 1), ("rc", 0), ("s3", 4, 1),
        ("s4", 3, 1), ("s4", 3, 2), ("s6", 3, 1), ("s6", 4, 1), ("rn", 1), ("rn", 0), ("s6", 3, 2), ("s6", 4, 2),
        ("re", 1), ("re", 0), ("fin", 1), ("fin", 0),
    ),
    (
        ("own", 1), ("put", 0), ("own", 0), ("mul", 0, 2), ("s1", 0, 2), ("zz", 0, 2), ("xf", 1), ("zz", 0, 3),
        ("s2", 0, 2), ("zz", 0, 0), ("xf", 0), ("zz", 0, 1), ("put", 1), ("put", 2), ("mul", 1, 2), ("xnear",),
        ("mul", 0, 1), ("s3", 0, 2), ("mul", 1, 1), ("zz", 1, 2), ("s1", 1, 2), ("s1", 0, 1), ("zz", 1, 3),
        ("s1", 1, 1), ("xlast",), ("mul", 0, 0), ("mul", 1, 0), ("s4", 0, 2), ("zz", 1, 0), ("s1", 0, 0),
        ("s2", 1, 2), ("s1", 1, 0), ("s2", 0, 1), ("zz", 1, 1), ("put", 4), ("put", 3), ("mul", 2), ("s2", 1, 1),
        ("zz", 2, 2), ("s2", 0, 0), ("s1", 2, 0), ("s1", 2, 1), ("s1", 2, 2), ("s3", 1, 2), ("zz", 2, 3),
        ("s2", 1, 0), ("s3", 0, 1), ("zz", 2, 0), ("s3", 1, 1), ("s3", 0, 0), ("s2", 2, 0), ("zz", 2, 1),
        ("put", 5), ("put", 6), ("mul", 3), ("s2", 2, 2), ("s2", 2, 1), ("s4", 1, 2), ("s3", 1, 0), ("s4", 0, 1),
        ("s1", 3, 0), ("s1", 3, 1), ("s1", 3, 2), ("s4", 1, 1), ("s4", 0, 0), ("put", 7), ("mul", 4), ("s3", 2, 0),
        ("s3", 2, 2), ("s6", 0), ("s6", 1, 2), ("s1", 4, 2), ("s1", 4, 0), ("s6", 1, 1), ("s4", 1, 0), ("s2", 3, 0),
        ("s1", 4, 1), ("s3", 2, 1), ("s2", 3, 1), ("s2", 3, 2), ("s6", 1, 0), ("s4", 2, 0), ("s4", 2, 2),
        ("s2", 4, 2), ("s2", 4, 0), ("s6", 2, 0), ("s3", 3, 0), ("s6", 2, 2), ("s2", 4, 1), ("s4", 2, 1),
        ("s3", 3, 1), ("s3", 3, 2), ("s3", 4, 2), ("s6", 2, 1), ("s3", 4, 0), ("s4", 3, 0), ("s3", 4, 1),
        ("s6", 3, 0), ("s6", 4, 0), ("rc", 0), ("rc", 1), ("s4", 3, 1), ("s4", 3, 2), ("s6", 3, 1), ("s6", 4, 1),
        ("rn", 0), ("rn", 1), ("s6", 3, 2), ("s6", 4, 2), ("re", 0), ("re", 1), ("fin", 0), ("fin", 1),
    ),
)


def split(value):
    high = value.astype(BF)
    return high, (value - high.astype(F32)).astype(BF)


def three(dim, a, b):
    a = jnp.concatenate([a[0], a[1], a[0]], axis=dim)
    b = jnp.concatenate([b[0], b[0], b[1]], axis=0)
    return lax.dot_general(a, b, (((dim,), (0,)), ((), ())), preferred_element_type=F32)


def lanes_of(s):
    first, n = LANES[s]
    return slice(first * STRIP, (first + n) * STRIP)


def kernel(m_ref, o_ref, block, panel, block_hi, block_lo, panel_hi, panel_lo, square_hi, square_lo, *refs):
    ns = len(SETS)
    part, from_core, mine, first_in, ours, second_in, square = (refs[k * ns : (k + 1) * ns] for k in range(7))
    (
        cube, x_chain, x_ended, factor, sums_y, sums_z,
        z_send, z_recv, x_send, x_recv, r_send, r_recv, g_send, g_recv, s_send, s_recv, local_sem,
    ) = refs[7 * ns :]
    y, c, x, z = (lax.axis_index(name) for name in ("y", "c", "x", "z"))

    def turn(name, here, by, size):
        return {name: lax.rem(here + by, size)}

    up_z, down_z = turn("z", z, 1, NZ), turn("z", z, NZ - 1, NZ)
    up_x, down_x = turn("x", x, 1, NX), turn("x", x, NX - 1, NX)
    odd = lax.rem(y, 2)
    y_near, y_far = turn("y", y, NY + 1 - 2 * odd, NY), turn("y", y, NY - 1 + 2 * odd, NY)
    other_core = {"c": 1 - c}
    z_peers = [turn("z", z, d, NZ) for d in range(1, NZ)]
    y_peers = [{"y": lax.rem(y + d, NY), "c": lax.rem(c + e, NC)} for d in range(NY) for e in range(NC)][1:]

    barrier = pltpu.get_barrier_semaphore()
    peers = [up_x, down_x, up_z, down_z, y_near, y_far, other_core]
    for peer in peers:
        pl.semaphore_signal(barrier, inc=1, device_id=peer, device_id_type=pl.DeviceIdType.MESH)
    fetch = pltpu.make_async_copy(m_ref, block.at[0, 0], local_sem.at[0])
    fetch.start()
    with jax.named_scope("fetch"):
        fetch.wait()
    with jax.named_scope("barrier"):
        pl.semaphore_wait(barrier, len(peers))

    def copy(src, dst, send, recv, peer):
        return pltpu.make_async_remote_copy(
            src_ref=src, dst_ref=dst, send_sem=send, recv_sem=recv,
            device_id=peer, device_id_type=pl.DeviceIdType.MESH,
        )

    def go(made):
        made.start()

    def all_sent(ref, sem):
        copy(ref, ref, sem, local_sem.at[2], up_x).wait_send()

    def all_here(ref, sem):
        copy(ref, ref, local_sem.at[2], sem, up_x).wait_recv()

    low, high = pl.ds(0, SHALF), pl.ds(SHALF, SHALF)
    gray, top = lax.rem(lax.div(y + 1, 2), 2), lax.div(y, 2)

    def sub(half, which):
        return pl.ds(pl.multiple_of(half * SHALF + which * SQUARTER, SQUARTER), SQUARTER)


    def iteration(it):
        block_i, panel_i, cube_i = block.at[it], panel.at[it], cube.at[it]

        def piece_of(q):
            return pl.ds(q * PIECE, PIECE)

        def z_copy(src, dst, q, pair, i, peer):
            return copy(
                block_i.at[src, piece_of(q)], block_i.at[dst, piece_of(q)], z_send.at[it], z_recv.at[it, pair, i], peer
            )

        up_order, down_order = (0, 2, 1, 3), (2, 0, 3, 1)
        ups, downs = {}, {}
        for pair in range(3):
            for i in range(PIECES):
                q, d = up_order[i], down_order[i]
                ups[pair, i] = z_copy(max(2 * pair, 0), 2 * pair + 2, q, pair, i, up_z)
                downs[pair, i] = z_copy(max(2 * pair - 1, 0), 2 * pair + 1, d, pair, i, down_z)
        for i in (0, 2):
            ups[3, i] = z_copy(6, 7, up_order[i], 3, 0, up_z)
            downs[3, i] = z_copy(5, 7, down_order[i], 3, 0, down_z)

        def x_copy(src, dst, q, k, peer):
            return copy(src.at[piece_of(q)], panel_i.at[dst, piece_of(q)], x_send.at[it], x_recv.at[it, k], peer)

        x_up = [x_copy(block_i.at[0], 3, q, (0, 1, 2, 2)[q], up_x) for q in range(PIECES)]
        x_down = [x_copy(block_i.at[0], 1, q, (2, 2, 0, 1)[q], down_x) for q in range(PIECES)]
        x_far = [x_copy(panel_i.at[3 - 2 * (q // 2)], 2, q, 3, (up_x, down_x)[q // 2]) for q in range(PIECES)]
        pair_rows = pl.ds(0, 2 * PIECE)

        def put_panel(slot, value):
            at = {2: 0, 1: 1, 3: 2, 0: 3}[slot]
            columns = slice(at * STRIP, (at + 1) * STRIP)
            panel_hi[:, columns], panel_lo[:, columns] = split(value)

        def own(h):
            for q, d in ((h, 2 + h), (2 + h, h)):
                go(x_up[q])
                go(x_down[d])
                i = up_order.index(q)
                go(ups[0, i])
                go(downs[0, i])

        def zz(pair, i):
            all_here(block_i.at[0, pair_rows], z_recv.at[it, pair, i])
            if (pair + 1, i) in ups:
                go(ups[pair + 1, i])
                go(downs[pair + 1, i])

        def put(pos):
            if pos == 7:
                all_here(block_i.at[0], z_recv.at[it, 3, 0])
            columns = slice(pos * STRIP, (pos + 1) * STRIP)
            value = block[it, pos]
            block_hi[:, columns], block_lo[:, columns] = split(value)
            if pos == 0:
                put_panel(0, value)

        def xf(i):
            all_here(block_i.at[0, pair_rows], x_recv.at[it, i])
            go(x_far[i])
            go(x_far[2 + i])

        def xnear():
            all_here(block_i.at[0], x_recv.at[it, 2])
            put_panel(3, panel[it, 3])
            put_panel(1, panel[it, 1])

        def xlast():
            all_here(block_i.at[0], x_recv.at[it, 3])
            put_panel(2, panel[it, 2])

        unit_sems = {(g, s): 5 * (g * ns + s) for g in range(len(GROUPS)) for s in range(ns)}

        def unit(g, s):
            run = pl.ds(*GROUPS[g])
            every = slice(None)

            three_steps = g * ns + s < THREE_STEPS

            def made(k, src, dst, peer):
                kind = (0, 1, 1, 2, 2, 4, 3, 3)[k]
                to = 0 if kind in (0, 4) else 3 if not three_steps else 2 if kind == 2 else 1
                wide = 0 if kind == 4 and g in MERGED else s
                return copy(src, dst, g_send.at[it, to], g_recv.at[it, unit_sems[g, wide] + kind], peer)

            def rows(ref, which):
                return ref[s].at[it, run, which]

            sums = square[s].at[it, run, c]
            cs = dict(
                core=made(0, part[s].at[it, run, 1 - c], from_core[s].at[it, run], other_core),
                join=made(5, sums, sums, other_core),
            )
            if three_steps:
                one, two = (sub(0, 1 - gray), sub(1, 1 - top)), (sub(0, gray), sub(1, top))
                low_sums, high_sums = square[s].at[it, run, c, two[0]], square[s].at[it, run, c, two[1]]
                cs["low_three"] = made(6, low_sums, low_sums, y_near)
                cs["high_three"] = made(7, high_sums, high_sums, y_far)
            else:
                one = two = (low, high)
            cs["low_one"] = made(1, rows(mine, one[0]), rows(first_in, one[0]), y_near)
            cs["high_one"] = made(2, rows(mine, one[1]), rows(first_in, one[1]), y_far)
            cs["low_two"] = made(3, rows(ours, two[0]), rows(second_in, two[0]), y_far)
            cs["high_two"] = made(4, rows(ours, two[1]), rows(second_in, two[1]), y_near)
            cs["kept"] = two
            cs["moved"] = first_in[s].at[it, run, low] if three_steps else first_in[s].at[it, run]
            cs["sems"] = [g_recv.at[it, unit_sems[g, s] + kind] for kind in range(5)]
            return cs

        units = {(g, s): unit(g, s) for g in range(len(GROUPS)) for s in range(ns)}

        def strips(g):
            first, n = GROUPS[g]
            return range(first, first + n)

        def factors(g):
            first, n = GROUPS[g]
            columns = slice(first * STRIP, (first + n) * STRIP)
            return block_hi[:, columns], block_lo[:, columns]

        def mul(g, *which):
            first, n = GROUPS[g]
            columns = lanes_of(which[0]) if which else slice(0, NX * STRIP)
            got = three(0, factors(g), (panel_hi[:, columns], panel_lo[:, columns]))
            for s in which or range(ns):
                piece = got if which else got[:, lanes_of(s)]
                part[s][it, first : first + n] = piece.reshape(n, NC, SROWS, piece.shape[1])
                go(units[g, s]["core"])

        def s1(g, s):
            cs = units[g, s]
            cs["core"].wait_recv()
            for p in strips(g):
                mine[s][it, p] = part[s][it, p, c] + from_core[s][it, p]
            go(cs["low_one"])
            go(cs["high_one"])

        def s2(g, s):
            cs = units[g, s]
            all_here(cs["moved"], cs["sems"][1])
            for half, kept in zip(("low", "high"), cs["kept"]):
                for p in strips(g):
                    ours[s][it, p, kept] = mine[s][it, p, kept] + first_in[s][it, p, kept]
                go(cs[half + "_two"])

        def s3(g, s):
            cs = units[g, s]
            all_here(cs["moved"], cs["sems"][2])
            for half, kept in zip(("low", "high"), cs["kept"]):
                for p in strips(g):
                    square[s][it, p, c, kept] = ours[s][it, p, kept] + second_in[s][it, p, kept]
                if half + "_three" in cs:
                    go(cs[half + "_three"])
            if "low_three" not in cs:
                go(cs["join"])

        def s4(g, s):
            cs = units[g, s]
            all_here(cs["moved"], cs["sems"][3])
            go(cs["join"])

        def s6(g, *which):
            first, n = GROUPS[g]
            rows = slice(first * STRIP, (first + n) * STRIP)
            todo = which or range(ns)
            if g in MERGED:
                all_here(block_i.at[pl.ds(0, n), pl.ds(0, HALF)], units[g, 0]["sems"][4])
            for s in todo:
                if g not in MERGED:
                    units[g, s]["join"].wait_recv()
                value = square[s][it, first : first + n]
                value = value.reshape(n * STRIP, value.shape[-1])
                if it == 0:
                    f = factor[0:1, 0:1]
                    value = value * (f * f)
                square_hi[rows, lanes_of(s)], square_lo[rows, lanes_of(s)] = split(value)
            columns = lanes_of(which[0]) if which else slice(0, NX * STRIP)
            b = square_hi[rows, columns], square_lo[rows, columns]
            strip_columns = slice(first * STRIP, (first + n) * STRIP)
            slots = [slot for s in todo for slot in SETS[s]]
            parts = 2 if len(slots) <= 2 else 1
            for part_rows in (slice(k * ROWS // parts, (k + 1) * ROWS // parts) for k in range(parts)):
                a = block_hi[part_rows, strip_columns], block_lo[part_rows, strip_columns]
                got = three(1, a, b)
                for k, slot in enumerate(slots):
                    piece = got[:, k * STRIP : (k + 1) * STRIP]
                    if first == 0:
                        cube[it, slot, part_rows] = piece
                    else:
                        cube[it, slot, part_rows] += piece

        def reduce_copies(r):
            upper, lower = pl.ds(r * PIECE, PIECE), pl.ds(HALF + r * PIECE, PIECE)

            def made(k, slot, rows, dst, peer):
                return copy(cube_i.at[slot, rows], dst, r_send.at[it], r_recv.at[it, r, k // 2], peer)

            return dict(
                chain_up=made(0, 2, upper, x_chain.at[it, r, 0], up_x),
                chain_down=made(1, 2, lower, x_chain.at[it, r, 1], down_x),
                near_down=made(2, 3, upper, x_chain.at[it, r, 2], down_x),
                near_up=made(3, 1, lower, x_chain.at[it, r, 3], up_x),
                end_up=made(4, 1, upper, x_ended.at[it, r, 0], up_x),
                end_down=made(5, 3, lower, x_ended.at[it, r, 1], down_x),
                rows=(upper, lower),
            )

        reduces = [reduce_copies(r) for r in range(2)]

        def rc(r):
            go(reduces[r]["chain_up"])
            go(reduces[r]["chain_down"])

        def rn(r):
            go(reduces[r]["near_up"])
            go(reduces[r]["near_down"])

        def re(r):
            cs = reduces[r]
            all_here(block_i.at[0, pair_rows], r_recv.at[it, r, 0])
            for k, (slot, way) in enumerate(((1, "up"), (3, "down"))):
                cube[it, slot, cs["rows"][k]] += x_chain[it, r, k]
                go(cs["end_" + way])

        def fin(r):
            cs = reduces[r]
            all_here(block_i.at[0, pair_rows], r_recv.at[it, r, 1])
            all_here(block_i.at[0, pair_rows], r_recv.at[it, r, 2])
            for k in range(2):
                rows = cs["rows"][k]
                product = cube[it, 0, rows] + (x_ended[it, r, k] + x_chain[it, r, 2 + k])
                value = block[it, 0, rows]
                if it == 0:
                    f = factor[0:1, 0:1]
                    new = (1.5 * f) * value - (0.5 * f) * product
                else:
                    new = 1.5 * value - 0.5 * product
                if it == ITERS - 1:
                    o_ref[rows] = new
                else:
                    block[it + 1, 0, rows] = new

        sy, sz = {}, {}
        if it == 0:
            for k, peer in enumerate(y_peers, 1):
                sy[k] = copy(sums_y.at[0], sums_y.at[k], s_send.at[0], s_recv.at[0], peer)
            for k, peer in enumerate(z_peers, 1):
                sz[k] = copy(sums_z.at[0], sums_z.at[k], s_send.at[1], s_recv.at[1], peer)

        def sums1():
            tile = jnp.zeros((8, 128), F32)
            for v in (block[it, 0], panel[it, 1], panel[it, 2], panel[it, 3]):
                v = v.reshape(ROWS // 8, 8, STRIP)
                tile = tile + jnp.sum(v * v, axis=0)
            sums_y[0] = tile
            for made in sy.values():
                go(made)

        def sums2():
            all_here(sums_y.at[pl.ds(1, NY * NC - 1)], s_recv.at[0])
            sums_z[0] = jnp.sum(sums_y[...], axis=0)
            for made in sz.values():
                go(made)

        def sums3():
            all_here(sums_z.at[pl.ds(1, NZ - 1)], s_recv.at[1])
            total = jnp.sum(jnp.sum(sums_z[...], axis=0), keepdims=True)
            factor[...] = jnp.broadcast_to(jnp.sqrt(N / total), factor.shape)

        work = dict(
            own=own, zz=zz, put=put, xf=xf, xnear=xnear, xlast=xlast, mul=mul, s1=s1, s2=s2, s3=s3, s4=s4, s6=s6,
            rc=rc, rn=rn, re=re, fin=fin, sums1=sums1, sums2=sums2, sums3=sums3,
        )
        for name, *args in ORDER[it]:
            with jax.named_scope("_".join([f"i{it}", name, *map(str, args)])):
                work[name](*args)

    for it in range(ITERS):
        iteration(it)
    with jax.named_scope("sent"):
        slow = sum(LANES[s][1] * n for g, (_, n) in enumerate(GROUPS) for s in range(ns) if g * ns + s < THREE_STEPS)
        fast, slow = (NX * NZ - slow) // NX, slow // NX
        for it in range(ITERS):
            all_sent(block.at[it, pl.ds(0, NZ - 1)], z_send.at[it])
            all_sent(block.at[it, pl.ds(0, NX - 1)], x_send.at[it])
            all_sent(block.at[it, pl.ds(0, NX - 1)], r_send.at[it])
            all_sent(block.at[it], g_send.at[it, 0])
            all_sent(block.at[it, pl.ds(0, slow), pl.ds(0, HALF)], g_send.at[it, 1])
            all_sent(block.at[it, pl.ds(0, slow), pl.ds(0, PIECE)], g_send.at[it, 2])
            all_sent(block.at[it, pl.ds(0, fast)], g_send.at[it, 3])
        all_sent(sums_y.at[pl.ds(1, NY * NC - 1)], s_send.at[0])
        all_sent(sums_z.at[pl.ds(1, NZ - 1)], s_send.at[1])


def shards(matrix):
    dma = pltpu.SemaphoreType.DMA
    wide = NX * STRIP
    widths = [n * STRIP for _, n in LANES]

    def per_set(*shape):
        return [pltpu.VMEM((ITERS, NZ, *shape, width), F32) for width in widths]

    return pl.pallas_call(
        kernel,
        out_shape=pltpu.VMEM((ROWS, STRIP), F32),
        in_specs=[pl.BlockSpec(memory_space=pltpu.HBM)],
        out_specs=pl.BlockSpec(memory_space=pltpu.VMEM),
        scratch_shapes=[
            pltpu.VMEM((ITERS, NZ, ROWS, STRIP), F32),
            pltpu.VMEM((ITERS, NX, ROWS, STRIP), F32),
            pltpu.VMEM((ROWS, NZ * STRIP), BF),
            pltpu.VMEM((ROWS, NZ * STRIP), BF),
            pltpu.VMEM((ROWS, wide), BF),
            pltpu.VMEM((ROWS, wide), BF),
            pltpu.VMEM((NZ * STRIP, wide), BF),
            pltpu.VMEM((NZ * STRIP, wide), BF),
            *per_set(NC, SROWS),
            *per_set(SROWS),
            *per_set(SROWS),
            *per_set(SROWS),
            *per_set(SROWS),
            *per_set(SROWS),
            *per_set(NC, SROWS),
            pltpu.VMEM((ITERS, NX, ROWS, STRIP), F32),
            pltpu.VMEM((ITERS, 2, 4, PIECE, STRIP), F32),
            pltpu.VMEM((ITERS, 2, 2, PIECE, STRIP), F32),
            pltpu.VMEM((8, 128), F32),
            pltpu.VMEM((NY * NC, 8, 128), F32),
            pltpu.VMEM((NZ, 8, 128), F32),
            dma((ITERS,)),
            dma((ITERS, 4, PIECES)),
            dma((ITERS,)),
            dma((ITERS, 4)),
            dma((ITERS,)),
            dma((ITERS, 2, 3)),
            dma((ITERS, 4)),
            dma((ITERS, 5 * len(GROUPS) * len(SETS))),
            dma((2,)),
            dma((2,)),
            dma((3,)),
        ],
        compiler_params=pltpu.CompilerParams(
            collective_id=0, has_side_effects=True, vmem_limit_bytes=56 * 1024 * 1024
        ),
    )(matrix)


def solution(mesh):
    grid = Mesh(mesh.devices.reshape(NY, NC, NX, NZ), ("y", "c", "x", "z"))
    spec = P(("y", "c"), ("x", "z"))
    return jax.shard_map(shards, mesh=grid, in_specs=(spec,), out_specs=spec, check_vma=False)
```

time: 106 us -> 103 us (0.972)
  Pallas kernels: 104 us -> 102 us
    pallas_call x1, Pallas kernels: 104 us -> 102 us  [shards(): pl.pallas_call(kernel, out_shape=pltpu.VMEM((ROWS, STRIP), F32), in_specs...]
where the time goes in v4:
time: 103 us
  Pallas kernels  102 us (99%)
    pallas_call x1, Pallas kernels, shards(): pl.pallas_call(kernel, out_shape=pltpu.VMEM((ROWS, STRIP), F32), in_specs...  102 us

profile of v4, /device:TPU:1, one launch (start us, length us, event | category | flops | bytes accessed | tf_op | source)
XLA Modules:
  0.0 102.5 jit_solution(10789390625806749539)
XLA Ops:
  0.0 101.8 %shard_map.17 = f32[512,128]{1,0:T(8,128)S(1)} custom-call(f32[512,128]{1,0:T(8,128)} %m_ref.1), custom_call_target="tpu_custom_call" | custom-call | tf_op jit(solution)/shard_map/pallas_call | solution.py:438
  101.8 0.7 copy.3

commit v5 on v4

--- a/solution.py
+++ b/solution.py
@@ -26,39 +26,39 @@
 THREE_STEPS = 12
 ORDER = (
     (
-        ("own", 0), ("put", 0), ("mul", 0, 2), ("own", 1), ("s1", 0, 2), ("zz", 0, 0), ("xf", 0), ("s2", 0, 2),
+        ("own", 0), ("own", 1), ("put", 0), ("mul", 0, 2), ("s1", 0, 2), ("zz", 0, 0), ("xf", 0), ("s2", 0, 2),
         ("zz", 0, 1), ("zz", 0, 2), ("xf", 1), ("s3", 0, 2), ("zz", 0, 3), ("put", 1), ("put", 2), ("mul", 1, 2),
         ("xnear",), ("mul", 1, 1), ("mul", 0, 1), ("zz", 1, 0), ("s1", 1, 2), ("s4", 0, 2), ("s1", 1, 1),
         ("zz", 1, 1), ("s1", 0, 1), ("xlast",), ("sums1",), ("mul", 0, 0), ("mul", 1, 0), ("zz", 1, 2),
         ("s1", 0, 0), ("s2", 1, 2), ("s1", 1, 0), ("zz", 1, 3), ("put", 3), ("put", 4), ("mul", 2), ("s2", 1, 1),
         ("s2", 0, 1), ("zz", 2, 0), ("sums2",), ("s2", 0, 0), ("s1", 2, 0), ("s1", 2, 1), ("s1", 2, 2),
         ("s3", 1, 2), ("zz", 2, 1), ("s2", 1, 0), ("zz", 2, 2), ("s3", 1, 1), ("s3", 0, 1), ("s3", 0, 0),
-        ("s2", 2, 0), ("zz", 2, 3), ("put", 6), ("put", 5), ("mul", 3), ("s2", 2, 1), ("s2", 2, 2), ("s4", 1, 2),
+        ("s2", 2, 0), ("zz", 2, 3), ("put", 5), ("put", 6), ("mul", 3), ("s2", 2, 1), ("s2", 2, 2), ("s4", 1, 2),
         ("s3", 1, 0), ("s1", 3, 0), ("s4", 1, 1), ("sums3",), ("s4", 0, 1), ("s1", 3, 1), ("s1", 3, 2),
         ("s4", 0, 0), ("put", 7), ("mul", 4), ("s3", 2, 0), ("s6", 0), ("s3", 2, 1), ("s6", 1, 1), ("s6", 1, 2),
         ("s2", 3, 0), ("s4", 1, 0), ("s1", 4, 0), ("s1", 4, 2), ("s3", 2, 2), ("s1", 4, 1), ("s2", 3, 1),
         ("s2", 3, 2), ("s6", 1, 0), ("s4", 2, 0), ("s4", 2, 1), ("s3", 3, 0), ("s6", 2, 0), ("s2", 4, 0),
         ("s2", 4, 2), ("s6", 2, 1), ("s4", 2, 2), ("s2", 4, 1), ("s3", 3, 1), ("s6", 2, 2), ("s3", 3, 2),
         ("s4", 3, 0), ("s3", 4, 0), ("s3", 4, 2), ("s6", 3, 0), ("s6", 4, 0), ("rc", 1), ("rc", 0), ("s3", 4, 1),
-        ("s4", 3, 1), ("s4", 3, 2), ("s6", 3, 1), ("s6", 4, 1), ("rn", 1), ("rn", 0), ("s6", 3, 2), ("s6", 4, 2),
+        ("s4", 3, 1), ("s4", 3, 2), ("s6", 3, 1), ("s6", 4, 1), ("rn", 0), ("s6", 3, 2), ("s6", 4, 2), ("rn", 1),
         ("re", 1), ("re", 0), ("fin", 1), ("fin", 0),
     ),
     (
-        ("own", 1), ("put", 0), ("own", 0), ("mul", 0, 2), ("s1", 0, 2), ("zz", 0, 2), ("xf", 1), ("zz", 0, 3),
+        ("own", 1), ("put", 0), ("mul", 0, 2), ("own", 0), ("s1", 0, 2), ("zz", 0, 2), ("xf", 1), ("zz", 0, 3),
         ("s2", 0, 2), ("zz", 0, 0), ("xf", 0), ("zz", 0, 1), ("put", 1), ("put", 2), ("mul", 1, 2), ("xnear",),
         ("mul", 0, 1), ("s3", 0, 2), ("mul", 1, 1), ("zz", 1, 2), ("s1", 1, 2), ("s1", 0, 1), ("zz", 1, 3),
         ("s1", 1, 1), ("xlast",), ("mul", 0, 0), ("mul", 1, 0), ("s4", 0, 2), ("zz", 1, 0), ("s1", 0, 0),
         ("s2", 1, 2), ("s1", 1, 0), ("s2", 0, 1), ("zz", 1, 1), ("put", 4), ("put", 3), ("mul", 2), ("s2", 1, 1),
         ("zz", 2, 2), ("s2", 0, 0), ("s1", 2, 0), ("s1", 2, 1), ("s1", 2, 2), ("s3", 1, 2), ("zz", 2, 3),
         ("s2", 1, 0), ("s3", 0, 1), ("zz", 2, 0), ("s3", 1, 1), ("s3", 0, 0), ("s2", 2, 0), ("zz", 2, 1),
-        ("put", 5), ("put", 6), ("mul", 3), ("s2", 2, 2), ("s2", 2, 1), ("s4", 1, 2), ("s3", 1, 0), ("s4", 0, 1),
+        ("put", 6), ("put", 5), ("mul", 3), ("s2", 2, 1), ("s2", 2, 2), ("s4", 1, 2), ("s3", 1, 0), ("s4", 0, 1),
         ("s1", 3, 0), ("s1", 3, 1), ("s1", 3, 2), ("s4", 1, 1), ("s4", 0, 0), ("put", 7), ("mul", 4), ("s3", 2, 0),
-        ("s3", 2, 2), ("s6", 0), ("s6", 1, 2), ("s1", 4, 2), ("s1", 4, 0), ("s6", 1, 1), ("s4", 1, 0), ("s2", 3, 0),
-        ("s1", 4, 1), ("s3", 2, 1), ("s2", 3, 1), ("s2", 3, 2), ("s6", 1, 0), ("s4", 2, 0), ("s4", 2, 2),
-        ("s2", 4, 2), ("s2", 4, 0), ("s6", 2, 0), ("s3", 3, 0), ("s6", 2, 2), ("s2", 4, 1), ("s4", 2, 1),
-        ("s3", 3, 1), ("s3", 3, 2), ("s3", 4, 2), ("s6", 2, 1), ("s3", 4, 0), ("s4", 3, 0), ("s3", 4, 1),
-        ("s6", 3, 0), ("s6", 4, 0), ("rc", 0), ("rc", 1), ("s4", 3, 1), ("s4", 3, 2), ("s6", 3, 1), ("s6", 4, 1),
-        ("rn", 0), ("rn", 1), ("s6", 3, 2), ("s6", 4, 2), ("re", 0), ("re", 1), ("fin", 0), ("fin", 1),
+        ("s6", 0), ("s3", 2, 1), ("s6", 1, 1), ("s6", 1, 2), ("s4", 1, 0), ("s3", 2, 2), ("s2", 3, 0), ("s1", 4, 0),
+        ("s1", 4, 2), ("s1", 4, 1), ("s2", 3, 1), ("s2", 3, 2), ("s6", 1, 0), ("s4", 2, 0), ("s4", 2, 1),
+        ("s4", 2, 2), ("s6", 2, 0), ("s3", 3, 0), ("s2", 4, 0), ("s6", 2, 1), ("s2", 4, 2), ("s6", 2, 2),
+        ("s2", 4, 1), ("s3", 3, 1), ("s3", 3, 2), ("s4", 3, 0), ("s3", 4, 0), ("s3", 4, 2), ("s6", 3, 0),
+        ("s6", 4, 0), ("rc", 0), ("rc", 1), ("s3", 4, 1), ("s4", 3, 1), ("s4", 3, 2), ("s6", 3, 1), ("s6", 4, 1),
+        ("rn", 1), ("rn", 0), ("s6", 3, 2), ("s6", 4, 2), ("re", 0), ("re", 1), ("fin", 0), ("fin", 1),
     ),
 )
 
@@ -204,7 +204,11 @@
             all_here(block_i.at[0], x_recv.at[it, 3])
             put_panel(2, panel[it, 2])
 
-        unit_sems = {(g, s): 5 * (g * ns + s) for g in range(len(GROUPS)) for s in range(ns)}
+        unit_sems, count = {}, 0
+        for g in range(len(GROUPS)):
+            for s in range(ns):
+                unit_sems[g, s] = count
+                count += 5
 
         def unit(g, s):
             run = pl.ds(*GROUPS[g])
@@ -216,7 +220,7 @@
                 kind = (0, 1, 1, 2, 2, 4, 3, 3)[k]
                 to = 0 if kind in (0, 4) else 3 if not three_steps else 2 if kind == 2 else 1
                 wide = 0 if kind == 4 and g in MERGED else s
-                return copy(src, dst, g_send.at[it, to], g_recv.at[it, unit_sems[g, wide] + kind], peer)
+                return copy(src, dst, g_send.at[it, to], g_recv.at[unit_sems[g, wide] + kind], peer)
 
             def rows(ref, which):
                 return ref[s].at[it, run, which]
@@ -239,7 +243,7 @@
             cs["high_two"] = made(4, rows(ours, two[1]), rows(second_in, two[1]), y_near)
             cs["kept"] = two
             cs["moved"] = first_in[s].at[it, run, low] if three_steps else first_in[s].at[it, run]
-            cs["sems"] = [g_recv.at[it, unit_sems[g, s] + kind] for kind in range(5)]
+            cs["sems"] = [g_recv.at[unit_sems[g, s] + kind] for kind in range(5)]
             return cs
 
         units = {(g, s): unit(g, s) for g in range(len(GROUPS)) for s in range(ns)}
@@ -469,7 +473,7 @@
             dma((ITERS,)),
             dma((ITERS, 2, 3)),
             dma((ITERS, 4)),
-            dma((ITERS, 5 * len(GROUPS) * len(SETS))),
+            dma((5 * len(GROUPS) * len(SETS),)),
             dma((2,)),
             dma((2,)),
             dma((3,)),

time: 103 us -> 101 us (0.981)
    pallas_call x1, Pallas kernels: 102 us -> 101 us  [shards(): pl.pallas_call(kernel, out_shape=pltpu.VMEM((ROWS, STRIP), F32), in_specs...]
where the time goes in v5:
time: 101 us
  Pallas kernels  101 us (100%)
    pallas_call x1, Pallas kernels, shards(): pl.pallas_call(kernel, out_shape=pltpu.VMEM((ROWS, STRIP), F32), in_specs...  101 us

profile of v5, /device:TPU:1, one launch (start us, length us, event | category | flops | bytes accessed | tf_op | source)
XLA Modules:
  0.0 101.3 jit_solution(16703241196085673525)
XLA Ops:
  0.0 100.6 %shard_map.17 = f32[512,128]{1,0:T(8,128)S(1)} custom-call(f32[512,128]{1,0:T(8,128)} %m_ref.1), custom_call_target="tpu_custom_call" | custom-call | tf_op jit(solution)/shard_map/pallas_call | solution.py:442
  100.6 0.7 copy.3

commit v6 on v5

--- a/solution.py
+++ b/solution.py
@@ -120,10 +120,10 @@
         made.start()
 
     def all_sent(ref, sem):
-        copy(ref, ref, sem, local_sem.at[2], up_x).wait_send()
+        copy(ref, ref, sem, local_sem.at[1], up_x).wait_send()
 
     def all_here(ref, sem):
-        copy(ref, ref, local_sem.at[2], sem, up_x).wait_recv()
+        copy(ref, ref, local_sem.at[1], sem, up_x).wait_recv()
 
     low, high = pl.ds(0, SHALF), pl.ds(SHALF, SHALF)
     gray, top = lax.rem(lax.div(y + 1, 2), 2), lax.div(y, 2)
@@ -140,7 +140,7 @@
 
         def z_copy(src, dst, q, pair, i, peer):
             return copy(
-                block_i.at[src, piece_of(q)], block_i.at[dst, piece_of(q)], z_send.at[it], z_recv.at[it, pair, i], peer
+                block_i.at[src, piece_of(q)], block_i.at[dst, piece_of(q)], z_send.at[it], z_recv.at[it, PIECES * pair + i], peer
             )
 
         up_order, down_order = (0, 2, 1, 3), (2, 0, 3, 1)
@@ -155,7 +155,7 @@
             downs[3, i] = z_copy(5, 7, down_order[i], 3, 0, down_z)
 
         def x_copy(src, dst, q, k, peer):
-            return copy(src.at[piece_of(q)], panel_i.at[dst, piece_of(q)], x_send.at[it], x_recv.at[it, k], peer)
+            return copy(src.at[piece_of(q)], panel_i.at[dst, piece_of(q)], x_send.at[it], x_recv.at[k], peer)
 
         x_up = [x_copy(block_i.at[0], 3, q, (0, 1, 2, 2)[q], up_x) for q in range(PIECES)]
         x_down = [x_copy(block_i.at[0], 1, q, (2, 2, 0, 1)[q], down_x) for q in range(PIECES)]
@@ -176,14 +176,14 @@
                 go(downs[0, i])
 
         def zz(pair, i):
-            all_here(block_i.at[0, pair_rows], z_recv.at[it, pair, i])
+            all_here(block_i.at[0, pair_rows], z_recv.at[it, PIECES * pair + i])
             if (pair + 1, i) in ups:
                 go(ups[pair + 1, i])
                 go(downs[pair + 1, i])
 
         def put(pos):
             if pos == 7:
-                all_here(block_i.at[0], z_recv.at[it, 3, 0])
+                all_here(block_i.at[0], z_recv.at[it, 3 * PIECES])
             columns = slice(pos * STRIP, (pos + 1) * STRIP)
             value = block[it, pos]
             block_hi[:, columns], block_lo[:, columns] = split(value)
@@ -191,24 +191,24 @@
                 put_panel(0, value)
 
         def xf(i):
-            all_here(block_i.at[0, pair_rows], x_recv.at[it, i])
+            all_here(block_i.at[0, pair_rows], x_recv.at[i])
             go(x_far[i])
             go(x_far[2 + i])
 
         def xnear():
-            all_here(block_i.at[0], x_recv.at[it, 2])
+            all_here(block_i.at[0], x_recv.at[2])
             put_panel(3, panel[it, 3])
             put_panel(1, panel[it, 1])
 
         def xlast():
-            all_here(block_i.at[0], x_recv.at[it, 3])
+            all_here(block_i.at[0], x_recv.at[3])
             put_panel(2, panel[it, 2])
 
         unit_sems, count = {}, 0
         for g in range(len(GROUPS)):
             for s in range(ns):
                 unit_sems[g, s] = count
-                count += 5
+                count += 4
 
         def unit(g, s):
             run = pl.ds(*GROUPS[g])
@@ -217,9 +217,9 @@
             three_steps = g * ns + s < THREE_STEPS
 
             def made(k, src, dst, peer):
-                kind = (0, 1, 1, 2, 2, 4, 3, 3)[k]
-                to = 0 if kind in (0, 4) else 3 if not three_steps else 2 if kind == 2 else 1
-                wide = 0 if kind == 4 and g in MERGED else s
+                kind = (0, 1, 1, 2, 2, 3, 1, 1)[k]
+                to = 0 if kind in (0, 3) else 3 if not three_steps else 2 if kind == 2 else 1
+                wide = 0 if kind == 3 and g in MERGED else s
                 return copy(src, dst, g_send.at[it, to], g_recv.at[unit_sems[g, wide] + kind], peer)
 
             def rows(ref, which):
@@ -243,7 +243,7 @@
             cs["high_two"] = made(4, rows(ours, two[1]), rows(second_in, two[1]), y_near)
             cs["kept"] = two
             cs["moved"] = first_in[s].at[it, run, low] if three_steps else first_in[s].at[it, run]
-            cs["sems"] = [g_recv.at[unit_sems[g, s] + kind] for kind in range(5)]
+            cs["sems"] = [g_recv.at[unit_sems[g, s] + kind] for kind in range(4)]
             return cs
 
         units = {(g, s): unit(g, s) for g in range(len(GROUPS)) for s in range(ns)}
@@ -295,7 +295,7 @@
 
         def s4(g, s):
             cs = units[g, s]
-            all_here(cs["moved"], cs["sems"][3])
+            all_here(cs["moved"], cs["sems"][1])
             go(cs["join"])
 
         def s6(g, *which):
@@ -303,7 +303,7 @@
             rows = slice(first * STRIP, (first + n) * STRIP)
             todo = which or range(ns)
             if g in MERGED:
-                all_here(block_i.at[pl.ds(0, n), pl.ds(0, HALF)], units[g, 0]["sems"][4])
+                all_here(block_i.at[pl.ds(0, n), pl.ds(0, HALF)], units[g, 0]["sems"][3])
             for s in todo:
                 if g not in MERGED:
                     units[g, s]["join"].wait_recv()
@@ -332,7 +332,7 @@
             upper, lower = pl.ds(r * PIECE, PIECE), pl.ds(HALF + r * PIECE, PIECE)
 
             def made(k, slot, rows, dst, peer):
-                return copy(cube_i.at[slot, rows], dst, r_send.at[it], r_recv.at[it, r, k // 2], peer)
+                return copy(cube_i.at[slot, rows], dst, r_send.at[it], r_recv.at[r, k // 2], peer)
 
             return dict(
                 chain_up=made(0, 2, upper, x_chain.at[it, r, 0], up_x),
@@ -356,15 +356,15 @@
 
         def re(r):
             cs = reduces[r]
-            all_here(block_i.at[0, pair_rows], r_recv.at[it, r, 0])
+            all_here(block_i.at[0, pair_rows], r_recv.at[r, 0])
             for k, (slot, way) in enumerate(((1, "up"), (3, "down"))):
                 cube[it, slot, cs["rows"][k]] += x_chain[it, r, k]
                 go(cs["end_" + way])
 
         def fin(r):
             cs = reduces[r]
-            all_here(block_i.at[0, pair_rows], r_recv.at[it, r, 1])
-            all_here(block_i.at[0, pair_rows], r_recv.at[it, r, 2])
+            all_here(block_i.at[0, pair_rows], r_recv.at[r, 1])
+            all_here(block_i.at[0, pair_rows], r_recv.at[r, 2])
             for k in range(2):
                 rows = cs["rows"][k]
                 product = cube[it, 0, rows] + (x_ended[it, r, k] + x_chain[it, r, 2 + k])
@@ -467,16 +467,16 @@
             pltpu.VMEM((NY * NC, 8, 128), F32),
             pltpu.VMEM((NZ, 8, 128), F32),
             dma((ITERS,)),
-            dma((ITERS, 4, PIECES)),
+            dma((ITERS, 3 * PIECES + 1)),
             dma((ITERS,)),
+            dma((4,)),
+            dma((ITERS,)),
+            dma((2, 3)),
             dma((ITERS, 4)),
-            dma((ITERS,)),
-            dma((ITERS, 2, 3)),
-            dma((ITERS, 4)),
-            dma((5 * len(GROUPS) * len(SETS),)),
+            dma((4 * len(GROUPS) * len(SETS),)),
             dma((2,)),
             dma((2,)),
-            dma((3,)),
+            dma((2,)),
         ],
         compiler_params=pltpu.CompilerParams(
             collective_id=0, has_side_effects=True, vmem_limit_bytes=56 * 1024 * 1024

time: 101 us -> 101 us (level)
  no operation moved by 1% of the time
where the time goes in v6:
time: 101 us
  Pallas kernels  100 us (99%)
    pallas_call x1, Pallas kernels, shards(): pl.pallas_call(kernel, out_shape=pltpu.VMEM((ROWS, STRIP), F32), in_specs...  100 us

profile of v6, /device:TPU:1, one launch (start us, length us, event | category | flops | bytes accessed | tf_op | source)
XLA Modules:
  0.0 101.0 jit_solution(161677382302718713)
XLA Ops:
  0.0 100.3 %shard_map.17 = f32[512,128]{1,0:T(8,128)S(1)} custom-call(f32[512,128]{1,0:T(8,128)} %m_ref.1), custom_call_target="tpu_custom_call" | custom-call | tf_op jit(solution)/shard_map/pallas_call | solution.py:442
  100.3 0.7 copy.3
